TPU v7x, 1024 devices: a whole 8x8x8 slice. The times are simulated.
1024 devices in a mesh: gx: 8 (over z_hi, core), gy: 16 (over z_lo, y), gz: 8 (over x).
Axes of the slice: x: 8, y: 8, z: 8 (z_hi: 4, z_lo: 2; z = z_hi * 2 + z_lo), core: 2. Of those that a mesh axis runs over, the one named last changes fastest.
Arguments:
- grads: bfloat16 [1024, 4, 1, 32, 3584], P(('gx', 'gy', 'gz')), may hold values from -1196032 to 1196032
- counts: int32 [1024], P(('gx', 'gy', 'gz')), may hold values from 1 to 4
- total_tokens: int32 [1], replicated, may hold values from 4000000 to 15999999
- master: float32 [1, 32, 3584], P(None, 'gy', ('gx', 'gz')), may hold values from -6 to 6
- moment1: float32 [1, 32, 3584], P(None, 'gy', ('gx', 'gz')), may hold values from -2 to 2
- moment2: float32 [1, 32, 3584], P(None, 'gy', ('gx', 'gz')), may hold values from 0.01 to 1
Outputs:
- params: bfloat16 [1, 32, 3584], replicated
- master_out: float32 [1, 32, 3584], P(None, 'gy', ('gx', 'gz'))
- moment1_out: float32 [1, 32, 3584], P(None, 'gy', ('gx', 'gz'))
- moment2_out: float32 [1, 32, 3584], P(None, 'gy', ('gx', 'gz'))
All inputs are finite; a program needn't handle non-finite values.
Results may differ from a plain program's by a relative error of at most 0.0004.
Values may be sent and summed in bfloat16 or wider, within the bound.
No kernel may reach another device: no remote copies, remote signals or barrier semaphores. Data moves between devices by JAX's collectives and lax.ppermute only.
A program may use at most 32 MiB of HBM per device.

v0:
```python
import jax
import jax.numpy as jnp
from jax import lax
from jax.sharding import PartitionSpec as P


def cut_along(shard, dim, peers):
    before, after = (shard.shape[:dim], shard.shape[dim + 1 :])
    return jnp.moveaxis(shard.reshape(*before, peers, -1, *after), dim, 0)


def summed_on_arrival(shard, axis, dim):
    peers = lax.axis_size(axis)
    parts = lax.all_to_all(cut_along(shard, dim, peers), axis, 0, 0, tiled=True)
    return jnp.sum(parts, axis=0)


def sent_to_all(shard, axis):
    copies = jnp.broadcast_to(shard, (lax.axis_size(axis), *shard.shape))
    return lax.all_to_all(copies, axis, split_axis=0, concat_axis=0, tiled=True)


def joined_along(parts, dim):
    parts = jnp.moveaxis(parts, 0, dim)
    shape = parts.shape
    return parts.reshape(*shape[:dim], shape[dim] * shape[dim + 1], *shape[dim + 2 :])


def collect(shard, axis, dim):
    parts = sent_to_all(shard, axis)
    return joined_along(parts, dim)


def body(grads, counts, total_tokens, master, moment1, moment2):
    rank_grads = grads[0]
    slots = jnp.arange(rank_grads.shape[0], dtype=jnp.int32)
    weights = (slots < counts[0]).astype(jnp.float32)
    accumulated = jnp.zeros(rank_grads.shape[1:], jnp.float32)
    for slot in range(rank_grads.shape[0]):
        accumulated = accumulated + weights[slot] * rank_grads[slot].astype(jnp.float32)
    partial_value = summed_on_arrival(accumulated, "gy", 1)
    summed = summed_on_arrival(partial_value, ("gx", "gz"), 2)
    gradient = summed / total_tokens.astype(jnp.float32)[0]
    moment1_out = 0.9 * moment1 + 0.1 * gradient
    moment2_out = 0.95 * moment2 + 0.05 * gradient * gradient
    first_fix = 1.0 - 0.9**10
    second_fix = 1.0 - 0.95**10
    update = moment1_out / first_fix / (jnp.sqrt(moment2_out / second_fix) + 1e-08)
    master_out = master - 0.01 * (update + 0.1 * master)
    shard_params = master_out.astype(jnp.bfloat16)
    wide_params = collect(shard_params, ("gx", "gz"), 2)
    params = collect(wide_params, "gy", 1)
    return (params, master_out, moment1_out, moment2_out)


def solution(mesh):
    return jax.shard_map(
        body,
        mesh=mesh,
        in_specs=(
            P(("gx", "gy", "gz"), None, None, None, None),
            P(("gx", "gy", "gz")),
            P(),
            P(None, "gy", ("gx", "gz")),
            P(None, "gy", ("gx", "gz")),
            P(None, "gy", ("gx", "gz")),
        ),
        out_specs=(
            P(),
            P(None, "gy", ("gx", "gz")),
            P(None, "gy", ("gx", "gz")),
            P(None, "gy", ("gx", "gz")),
        ),
        check_vma=False,
    )
```

profile of v0, /device:TPU:16, one launch (start us, length us, event | category | flops | bytes accessed | tf_op | source)
XLA Modules:
  0.0 97.1 jit_solution(8825072722994273549)
XLA Ops:
  1.3 0.6 fusion.4
  1.9 4.0 %multiply_add_fusion = f32[1,1,1,32,3584]{4,3,2,1,0:T(8,128)S(1)} fusion(bf16[1,4,1,32,3584]{4,3,2,1,0:T(8,128)(2,1)} %param.6, f32[]{:T(128)} %bitcast.4, f32[]{:T(128)} %bitcast.3, f32[]{:T(128)} %bitcast.2, f32[]{:T(128)} %bitcast.1), kind=kLoop, calls=%fused_computation | loop fusion | flops 1261568 | bytes 1376272 | tf_op jit(solution)/shard_map/add | solution.py:40
  5.9 0.3 reshape.149
  6.2 25.7 %all_to_all.20 = f32[16,1,2,3584]{3,2,1,0:T(2,128)S(1)} all-to-all(f32[16,1,2,3584]{3,2,1,0:T(2,128)S(1)} %reshape.149), channel_id=1, replica_groups=mesh['gx'=8,'gy'=16,'gz'=8] {'gy'}, dimensions={0} | all-to-all | bytes 917504 | tf_op jit(solution)/shard_map/all_to_all | solution.py:14
  31.9 0.1 reduce_sum.18
  32.1 0.1 reshape.147
  32.2 0.7 copy.10
  32.8 19.2 %all-to-all-start.1 = ((f32[64,1,2,56]{3,2,1,0:T(2,128)}), f32[64,1,2,56]{3,2,1,0:T(2,128)S(1)}, u32[]{:S(2)}, u32[]{:S(2)}) async-start(f32[64,1,2,56]{3,2,1,0:T(2,128)} %copy.10), calls=%async_computation.1 | async-start | bytes 131072 | tf_op jit(solution)/shard_map/all_to_all | solution.py:14
  52.7 11.7 %all-to-all-done.1 = f32[64,1,2,56]{3,2,1,0:T(2,128)S(1)} async-done(((f32[64,1,2,56]{3,2,1,0:T(2,128)}), f32[64,1,2,56]{3,2,1,0:T(2,128)S(1)}, u32[]{:S(2)}, u32[]{:S(2)}) %all-to-all-start.1) | async-done | bytes 28704 | tf_op jit(solution)/shard_map/all_to_all | solution.py:14
  64.4 0.0 copy-start.1
  64.4 0.0 copy-start.2
  64.4 0.1 reduce_sum.19
  64.5 0.0 copy-start
  64.5 0.6 copy-done.1
  65.1 0.0 copy-done.2
  65.1 0.1 copy-done
  65.2 0.6 convert_bitcast_fusion
  65.8 15.8 %all_to_all.21 = bf16[64,1,2,56]{3,2,1,0:T(2,128)(2,1)S(1)} all-to-all(bf16[64,1,2,56]{3,2,1,0:T(2,128)(2,1)S(1)} %broadcast_in_dim.6), channel_id=1, replica_groups=mesh['gx'=8,'gy'=16,'gz'=8] {'gx','gz'}, dimensions={0} | all-to-all | bytes 28672 | tf_op jit(solution)/shard_map/all_to_all | solution.py:20
  81.6 0.1 reshape.148
  81.7 0.1 broadcast_in_dim.7
  81.9 14.5 %all_to_all.22 = bf16[16,1,2,3584]{3,2,1,0:T(2,128)(2,1)S(1)} all-to-all(bf16[16,1,2,3584]{3,2,1,0:T(2,128)(2,1)S(1)} %broadcast_in_dim.7), channel_id=1, replica_groups=mesh['gx'=8,'gy'=16,'gz'=8] {'gy'}, dimensions={0} | all-to-all | bytes 458752 | tf_op jit(solution)/shard_map/all_to_all | solution.py:20
  96.3 0.8 reshape_transpose.3
  (3 shorter events, 0.0 us)
Async XLA Ops:
  32.8 31.6 %all-to-all-start.1 = ((f32[64,1,2,56]{3,2,1,0:T(2,128)}), f32[64,1,2,56]{3,2,1,0:T(2,128)S(1)}, u32[]{:S(2)}, u32[]{:S(2)}) async-start(f32[64,1,2,56]{3,2,1,0:T(2,128)} %copy.10), calls=%async_computation.1 | async-start | bytes 131072 | tf_op jit(solution)/shard_map/all_to_all | solution.py:14
  64.4 0.7 copy-start.1
  64.4 0.7 copy-start.2
  64.5 0.7 copy-start
where the time goes:
time: 97.5 us; the launch traced here: 97.1 us
  blocking collectives  56 us (57%)
  starting transfers between devices  19.2 us (20%)
  waiting for transfers between devices  11.7 us (12%)
  other arithmetic  4.85 us (5%)
  local copies, waits for them, and re-layouts  3.36 us (3%)
  between operations  1.98 us (2%)
    all_to_all x2, blocking collectives, sent_to_all(): return lax.all_to_all(copies, axis, split_axis=0, concat_axis=0, tiled=True)  30.3 us
    all_to_all x1, blocking collectives, summed_on_arrival(): parts = lax.all_to_all(cut_along(shard, dim, peers), axis, 0, 0, tiled=True)  25.7 us
    all_to_all x1, starting transfers between devices, summed_on_arrival(): parts = lax.all_to_all(cut_along(shard, dim, peers), axis, 0, 0, tiled=True)  19.2 us
    all_to_all x1, waiting for transfers between devices, summed_on_arrival(): parts = lax.all_to_all(cut_along(shard, dim, peers), axis, 0, 0, tiled=True)  11.7 us
    add x1, other arithmetic, body(): accumulated + weights[slot] * rank_grads[slot].astype(jnp.float32)  4.03 us
  transfers between devices with their start and end apart: 1, of which 1 were waited for; matrix products, arithmetic and copies ran while one was open for 0% of the time, Pallas kernels for 0%

commit v1 on v0

v1 whole, which is shorter than its diff:
```python
import jax
import jax.numpy as jnp
from jax import lax
from jax.experimental import pallas as pl
from jax.experimental.pallas import tpu as pltpu
from jax.sharding import PartitionSpec as P

COLS = ("gx", "gz")
ROWS = "gy"
VMEM = pl.BlockSpec(memory_space=pltpu.VMEM)
SMEM = pl.BlockSpec(memory_space=pltpu.SMEM)
HBM = pl.BlockSpec(memory_space=pltpu.HBM)
CHUNKS = 4
PARAMS = pltpu.CompilerParams(vmem_limit_bytes=8 * 1024 * 1024)


def accumulate(counts, tokens, grads, master, moment1, moment2, out, state, slots, acc, sems, small):
    _, n_slots, _, rows, width = grads.shape
    peers, half, two_w = out.shape
    w = two_w // 2
    step = width // CHUNKS
    copies = [
        pltpu.make_async_copy(grads.at[0, :, 0, :, pl.ds(c * step, step)], slots.at[:, :, pl.ds(c * step, step)], sems.at[c])
        for c in range(CHUNKS)
    ]
    state_copies = [
        pltpu.make_async_copy(x.at[0], small.at[i], sems.at[CHUNKS + i]) for i, x in enumerate((master, moment1, moment2))
    ]
    for copy in copies:
        copy.start()
    for copy in state_copies:
        copy.start()
    count = counts[0]
    for c in range(CHUNKS):
        copies[c].wait()
        at = slice(c * step, (c + 1) * step)
        total = slots[0, :, at].astype(jnp.float32)
        for slot in range(1, n_slots):
            weight = (slot < count).astype(jnp.float32)
            total = total + weight * slots[slot, :, at].astype(jnp.float32)
        acc[:, at] = total
        for j in range(c * peers // CHUNKS, (c + 1) * peers // CHUNKS):
            out[j, :, :w] = acc[:half, j * w : (j + 1) * w]
            out[j, :, w:] = acc[half:, j * w : (j + 1) * w]
    for copy in state_copies:
        copy.wait()
    state[0:2, :w] = small[0]
    state[0:2, w:] = small[1]
    state[2:4, :w] = small[2]
    state[2:4, w:] = jnp.full((2, w), tokens[0].astype(jnp.float32))
    state[4:8, :] = jnp.zeros((4, two_w), jnp.float32)


def reduce_and_pack(parts, state, out):
    half = parts.shape[1]
    total = parts[0]
    for j in range(1, parts.shape[0]):
        total = total + parts[j]
    for j in range(out.shape[0]):
        out[j, :half, :] = total
        out[j, half:, :] = state[...]


def adam(parts, send, master_out, moment1_out, moment2_out, state, result):
    peers = parts.shape[0]
    half, two_w = send.shape[1:]
    w = two_w // 2
    total = parts[0, :half, :]
    for j in range(1, peers):
        total = total + parts[j, :half, :]
    for j in range(peers):
        h, y = divmod(j, peers // 2)
        at = slice(h * w, (h + 1) * w)
        state[0, 2 * y : 2 * y + 2, at] = parts[j, half : half + 2, :w]
        state[1, 2 * y : 2 * y + 2, at] = parts[j, half : half + 2, w:]
        state[2, 2 * y : 2 * y + 2, at] = parts[j, half + 2 : half + 4, :w]
    master, moment1, moment2 = state[0], state[1], state[2]
    gradient = total / parts[0, half + 2 : half + 3, w : w + 1]
    first = 0.9 * moment1 + 0.1 * gradient
    second = 0.95 * moment2 + 0.05 * gradient * gradient
    first_fix = 1.0 - 0.9**10
    second_fix = 1.0 - 0.95**10
    update = first / first_fix / (jnp.sqrt(second / second_fix) + 1e-08)
    new_master = master - 0.01 * (update + 0.1 * master)
    params = new_master.astype(jnp.bfloat16)
    for j in range(send.shape[0]):
        send[j] = params
    result[0], result[1], result[2] = new_master, first, second
    mine = lax.axis_index(ROWS)
    h, y = mine // (peers // 2), mine % (peers // 2)
    for i, out in enumerate((master_out, moment1_out, moment2_out)):
        rows = result[i, pl.ds(2 * y, 2), :]
        out[0] = jnp.where(h == 0, rows[:, :w], rows[:, w:])


def assemble(parts, out):
    peers, half, two_w = parts.shape
    w = two_w // 2
    for j in range(peers):
        out[0, :half, j * w : (j + 1) * w] = parts[j, :, :w]
        out[0, half:, j * w : (j + 1) * w] = parts[j, :, w:]


def body(grads, counts, total_tokens, master, moment1, moment2):
    f32, bf16 = jnp.float32, jnp.bfloat16
    rows, width = grads.shape[3:]
    n_cols, n_rows = lax.axis_size(COLS), lax.axis_size(ROWS)
    half, two_w = rows // 2, 2 * width // n_cols
    exchange = lambda x, axes: lax.all_to_all(x, axes, 0, 0, tiled=True)

    parts, state = pl.pallas_call(
        accumulate,
        out_shape=(jax.ShapeDtypeStruct((n_cols, half, two_w), f32), jax.ShapeDtypeStruct((8, two_w), f32)),
        in_specs=[SMEM] * 2 + [HBM] * 4,
        out_specs=(VMEM, VMEM),
        scratch_shapes=[
            pltpu.VMEM((grads.shape[1], rows, width), bf16),
            pltpu.VMEM((rows, width), f32),
            pltpu.SemaphoreType.DMA((CHUNKS + 3,)),
            pltpu.VMEM((3, *master.shape[1:]), f32),
        ],
        compiler_params=PARAMS,
    )(counts, total_tokens, *(pltpu.with_memory_space_constraint(x, pltpu.HBM) for x in (grads, master, moment1, moment2)))
    parts = exchange(parts, COLS)
    packed = pl.pallas_call(
        reduce_and_pack,
        out_shape=jax.ShapeDtypeStruct((n_rows, half + 8, two_w), f32),
        in_specs=[VMEM, VMEM],
        out_specs=VMEM,
        compiler_params=PARAMS,
    )(parts, state)
    packed = exchange(packed, ROWS)
    shard = jax.ShapeDtypeStruct(master.shape, f32)
    send, master_out, moment1_out, moment2_out = pl.pallas_call(
        adam,
        out_shape=(jax.ShapeDtypeStruct((n_cols, half, two_w), bf16), shard, shard, shard),
        in_specs=[VMEM],
        out_specs=(VMEM,) * 4,
        scratch_shapes=[pltpu.VMEM((3, half, two_w), f32), pltpu.VMEM((3, half, two_w), f32)],
        compiler_params=PARAMS,
    )(packed)
    gathered = exchange(send, COLS)
    params = pl.pallas_call(
        assemble,
        out_shape=jax.ShapeDtypeStruct((1, rows, width), bf16),
        in_specs=[VMEM],
        out_specs=VMEM,
        compiler_params=PARAMS,
    )(gathered)
    return (params, master_out, moment1_out, moment2_out)


def solution(mesh):
    state = P(None, "gy", ("gx", "gz"))
    return jax.shard_map(
        body,
        mesh=mesh,
        in_specs=(P(("gx", "gy", "gz"), None, None, None, None), P(("gx", "gy", "gz")), P(), state, state, state),
        out_specs=(P(), state, state, state),
        check_vma=False,
    )
```

time: 97.5 us -> 86.7 us (0.89)
  blocking collectives: 56 us -> 80.9 us
  starting transfers between devices: 19.2 us -> 0 us
  waiting for transfers between devices: 11.7 us -> 0 us
  other arithmetic: 4.85 us -> 0 us
  Pallas kernels: 0 us -> 3.59 us
  local copies, waits for them, and re-layouts: 3.36 us -> 0 us
    all_to_all x3, blocking collectives: 56 us -> 80.9 us  [body(): exchange = lambda x, axes: lax.all_to_all(x, axes, 0, 0, tiled=True)]
    all_to_all x1 -> x0, starting transfers between devices: 19.2 us -> none  [summed_on_arrival(): parts = lax.all_to_all(cut_along(shard, dim, peers), axis, 0, 0, tiled=True)]
    all_to_all x1 -> x0, waiting for transfers between devices: 11.7 us -> none  [summed_on_arrival(): parts = lax.all_to_all(cut_along(shard, dim, peers), axis, 0, 0, tiled=True)]
    add x1 -> x0, other arithmetic: 4.03 us -> none  [body(): accumulated + weights[slot] * rank_grads[slot].astype(jnp.float32)]
    pallas_call x0 -> x4, Pallas kernels: none -> 3.59 us  [the longest x1 1.73 us: body(): pl.pallas_call(accumulate, out_shape=(jax.ShapeDtypeStruct((n_cols, half,...]
  transfers between devices with their start and end apart: 1 -> 0, of which waited for: 1 -> 0; matrix products, arithmetic and copies ran while one was open for 0% -> 0% of each run, Pallas kernels for 0% -> 0%
where the time goes in v1:
time: 86.7 us; the launch traced here: 86.4 us
  blocking collectives  80.9 us (93%)
  Pallas kernels  3.59 us (4%)
  between operations  1.94 us (2%)
    all_to_all x3, blocking collectives, body(): exchange = lambda x, axes: lax.all_to_all(x, axes, 0, 0, tiled=True)  80.9 us

profile of v1, /device:TPU:16, one launch (start us, length us, event | category | flops | bytes accessed | tf_op | source)
XLA Modules:
  0.0 86.4 jit_solution(15654605428444163817)
XLA Ops:
  1.9 1.7 %shard_map.93 = (f32[64,16,112]{2,1,0:T(8,128)S(1)}, f32[8,112]{1,0:T(8,128)S(1)}) custom-call(s32[1]{0:T(128)S(6)} %copy.10.counts, s32[1]{0:T(128)S(6)} %copy.11.tokens, bf16[1,4,1,32,3584]{4,3,2,1,0:T(8,128)(2,1)} %grads.1, f32[1,2,56]{2,1,0:T(2,128)} %master.1, f32[1,2,56]{2,1,0:T(2,128)} %moment1.1, f32[1,2,56]{2,1,0:T(2,128)} %moment2.1), custom_call_target="tpu_custom_call" | custom-call | tf_op jit(solution)/shard_map/pallas_call | solution.py:111
  3.7 40.9 %all_to_all.15.parts = f32[64,16,112]{2,1,0:T(8,128)S(1)} all-to-all(f32[64,16,112]{2,1,0:T(8,128)S(1)} %get-tuple-element.10), channel_id=1, replica_groups=mesh['gx'=8,'gy'=16,'gz'=8] {'gx','gz'}, dimensions={0} | all-to-all | bytes 917504 | tf_op jit(solution)/shard_map/all_to_all | solution.py:109
  44.5 0.1 shard_map.94
  44.6 18.0 %all_to_all.16.parts = f32[16,24,112]{2,1,0:T(8,128)S(1)} all-to-all(f32[16,24,112]{2,1,0:T(8,128)S(1)} %shard_map.94), channel_id=1, replica_groups=mesh['gx'=8,'gy'=16,'gz'=8] {'gy'}, dimensions={0} | all-to-all | bytes 344064 | tf_op jit(solution)/shard_map/all_to_all | solution.py:109
  62.6 0.8 shard_map.95
  63.4 22.0 %all_to_all.17.parts = bf16[64,16,112]{2,1,0:T(8,128)(2,1)S(1)} all-to-all(bf16[64,16,112]{2,1,0:T(8,128)(2,1)S(1)} %get-tuple-element.12), channel_id=1, replica_groups=mesh['gx'=8,'gy'=16,'gz'=8] {'gx','gz'}, dimensions={0} | all-to-all | bytes 458752 | tf_op jit(solution)/shard_map/all_to_all | solution.py:109
  85.4 1.0 %shard_map.96 = bf16[1,32,3584]{2,1,0:T(8,128)(2,1)} custom-call(bf16[64,16,112]{2,1,0:T(8,128)(2,1)S(1)} %all_to_all.17.parts), custom_call_target="tpu_custom_call" | custom-call | tf_op jit(solution)/shard_map/pallas_call | solution.py:143

commit v2 on v1

v2 whole, which is shorter than its diff:
```python
import jax
import jax.numpy as jnp
from jax import lax
from jax.experimental import pallas as pl
from jax.experimental.pallas import tpu as pltpu
from jax.sharding import Mesh, PartitionSpec as P

PLANE = ("zh", "gy")
LINE = ("core", "gz")
VMEM = pl.BlockSpec(memory_space=pltpu.VMEM)
SMEM = pl.BlockSpec(memory_space=pltpu.SMEM)
HBM = pl.BlockSpec(memory_space=pltpu.HBM)
PARAMS = pltpu.CompilerParams(vmem_limit_bytes=8 * 1024 * 1024)


def accumulate(counts, tokens, grads, master, moment1, moment2, out, state, slots, acc, small, sems):
    _, n_slots, _, rows, width = grads.shape
    peers, _, block = out.shape
    chunks, n_rows = width // block, rows // 2
    copies = [
        pltpu.make_async_copy(grads.at[0, :, 0, :, pl.ds(c * block, block)], slots.at[:, :, pl.ds(c * block, block)], sems.at[c])
        for c in range(chunks)
    ]
    state_copies = [
        pltpu.make_async_copy(x.at[0], small.at[i], sems.at[chunks + i]) for i, x in enumerate((master, moment1, moment2))
    ]
    for copy in copies + state_copies:
        copy.start()
    count = counts[0]
    for c in range(chunks):
        copies[c].wait()
        at = slice(c * block, (c + 1) * block)
        total = slots[0, :, at].astype(jnp.float32)
        for slot in range(1, n_slots):
            weight = (slot < count).astype(jnp.float32)
            total = total + weight * slots[slot, :, at].astype(jnp.float32)
        acc[:, at] = total
        for i in range(n_rows):
            out[c * n_rows + i] = acc[2 * i : 2 * i + 2, at]
    for copy in state_copies:
        copy.wait()
    w = small.shape[-1]
    for i in range(3):
        state[:, i * w : (i + 1) * w] = small[i]
    state[:, 3 * w :] = jnp.full((2, state.shape[1] - 3 * w), tokens[0].astype(jnp.float32))


def reduce_and_pack(parts, state, out):
    block = parts.shape[2]
    total = parts[0]
    for j in range(1, parts.shape[0]):
        total = total + parts[j]
    for j in range(out.shape[0]):
        out[j, :, :block] = total
        out[j, :, block:] = state[...]


def adam(parts, send, master_out, moment1_out, moment2_out, state, result):
    peers = parts.shape[0]
    _, _, block = send.shape
    w = block // peers
    total = parts[0, :, :block]
    for j in range(1, peers):
        total = total + parts[j, :, :block]
    for j in range(peers):
        for i in range(3):
            state[i, :, j * w : (j + 1) * w] = parts[j, :, block + i * w : block + (i + 1) * w]
    master, moment1, moment2 = state[0], state[1], state[2]
    tokens = parts[0, 0:1, block + 3 * w : block + 3 * w + 1]
    gradient = total / tokens
    first = 0.9 * moment1 + 0.1 * gradient
    second = 0.95 * moment2 + 0.05 * gradient * gradient
    first_fix = 1.0 - 0.9**10
    second_fix = 1.0 - 0.95**10
    update = first / first_fix / (jnp.sqrt(second / second_fix) + 1e-08)
    new_master = master - 0.01 * (update + 0.1 * master)
    params = new_master.astype(jnp.bfloat16)
    for j in range(send.shape[0]):
        send[j] = params
    result[0], result[1], result[2] = new_master, first, second
    mine = lax.axis_index(LINE)
    for j in range(peers):

        @pl.when(mine == j)
        def _():
            for i, out in enumerate((master_out, moment1_out, moment2_out)):
                out[0] = result[i, :, j * w : (j + 1) * w]


def assemble(parts, out):
    peers, _, block = parts.shape
    n_rows = out.shape[1] // 2
    for j in range(peers):
        c, i = divmod(j, n_rows)
        out[0, 2 * i : 2 * i + 2, c * block : (c + 1) * block] = parts[j]


def body(grads, counts, total_tokens, master, moment1, moment2):
    f32, bf16 = jnp.float32, jnp.bfloat16
    n_slots, _, rows, width = grads.shape[1:]
    n_plane, n_line = lax.axis_size(PLANE), lax.axis_size(LINE)
    block, w = width // lax.axis_size("zh"), master.shape[2]
    extra = -(-(3 * w + 1) // 128) * 128
    exchange = lambda x, axes: lax.all_to_all(x, axes, 0, 0, tiled=True)
    pinned = [pltpu.with_memory_space_constraint(x, pltpu.HBM) for x in (grads, master, moment1, moment2)]

    parts, state = pl.pallas_call(
        accumulate,
        out_shape=(jax.ShapeDtypeStruct((n_plane, 2, block), f32), jax.ShapeDtypeStruct((2, extra), f32)),
        in_specs=[SMEM] * 2 + [HBM] * 4,
        out_specs=(VMEM, VMEM),
        scratch_shapes=[
            pltpu.VMEM((n_slots, rows, width), bf16),
            pltpu.VMEM((rows, width), f32),
            pltpu.VMEM((3, 2, w), f32),
            pltpu.SemaphoreType.DMA((width // block + 3,)),
        ],
        compiler_params=PARAMS,
    )(counts, total_tokens, *pinned)
    parts = exchange(parts, PLANE)
    packed = pl.pallas_call(
        reduce_and_pack,
        out_shape=jax.ShapeDtypeStruct((n_line, 2, block + extra), f32),
        in_specs=[VMEM, VMEM],
        out_specs=VMEM,
        compiler_params=PARAMS,
    )(parts, state)
    packed = exchange(packed, LINE)
    shard = jax.ShapeDtypeStruct(master.shape, f32)
    send, master_out, moment1_out, moment2_out = pl.pallas_call(
        adam,
        out_shape=(jax.ShapeDtypeStruct((n_plane, 2, block), bf16), shard, shard, shard),
        in_specs=[VMEM],
        out_specs=(VMEM,) * 4,
        scratch_shapes=[pltpu.VMEM((3, 2, block), f32), pltpu.VMEM((3, 2, block), f32)],
        compiler_params=PARAMS,
    )(packed)
    gathered = exchange(send, PLANE)
    params = pl.pallas_call(
        assemble,
        out_shape=jax.ShapeDtypeStruct((1, rows, width), bf16),
        in_specs=[VMEM],
        out_specs=VMEM,
        compiler_params=PARAMS,
    )(gathered)
    return (params, master_out, moment1_out, moment2_out)


def solution(mesh):
    gx, gy, gz = mesh.devices.shape
    fine = Mesh(mesh.devices.reshape(gx // 2, 2, gy, gz), ("zh", "core", "gy", "gz"))
    ranks = ("zh", "core", "gy", "gz")
    state = P(None, "gy", ("zh", "core", "gz"))
    return jax.shard_map(
        body,
        mesh=fine,
        in_specs=(P(ranks, None, None, None, None), P(ranks), P(), state, state, state),
        out_specs=(P(), state, state, state),
        check_vma=False,
    )
```

time: 86.7 us -> 81.1 us (0.935)
  the two profiles are of different devices: /device:TPU:16 before, /device:TPU:2 now
where the time goes in v2:
time: 81.1 us; the launch traced here: 80.9 us
  blocking collectives  75.7 us (93%)
  Pallas kernels  3.2 us (4%)
  between operations  1.94 us (2%)
    all_to_all x3, blocking collectives, body(): exchange = lambda x, axes: lax.all_to_all(x, axes, 0, 0, tiled=True)  75.7 us

profile of v2, /device:TPU:2, one launch (start us, length us, event | category | flops | bytes accessed | tf_op | source)
XLA Modules:
  0.0 80.9 jit_solution(6768518299611830536)
XLA Ops:
  1.9 1.5 %shard_map.93 = (f32[64,2,896]{2,1,0:T(2,128)S(1)}, f32[2,256]{1,0:T(2,128)S(1)}) custom-call(s32[1]{0:T(128)S(6)} %copy.10.counts, s32[1]{0:T(128)S(6)} %copy.11.tokens, bf16[1,4,1,32,3584]{4,3,2,1,0:T(8,128)(2,1)} %grads.1, f32[1,2,56]{2,1,0:T(2,128)} %master.1, f32[1,2,56]{2,1,0:T(2,128)} %moment1.1, f32[1,2,56]{2,1,0:T(2,128)} %moment2.1), custom_call_target="tpu_custom_call" | custom-call | tf_op jit(solution)/shard_map/pallas_call | solution.py:107
  3.4 41.6 %all_to_all.15.parts = f32[64,2,896]{2,1,0:T(2,128)S(1)} all-to-all(f32[64,2,896]{2,1,0:T(2,128)S(1)} %get-tuple-element.10), channel_id=1, replica_groups=mesh['zh'=4,'core'=2,'gy'=16,'gz'=8] {'zh','gy'}, dimensions={0} | all-to-all | bytes 917504 | tf_op jit(solution)/shard_map/all_to_all | solution.py:104
  45.1 0.1 shard_map.94
  45.1 15.6 %all_to_all.16.parts = f32[16,2,1152]{2,1,0:T(2,128)S(1)} all-to-all(f32[16,2,1152]{2,1,0:T(2,128)S(1)} %shard_map.94), channel_id=1, replica_groups=mesh['zh'=4,'core'=2,'gy'=16,'gz'=8] {'core','gz'}, dimensions={0} | all-to-all | bytes 294912 | tf_op jit(solution)/shard_map/all_to_all | solution.py:104
  60.8 0.8 %shard_map.95 = (bf16[64,2,896]{2,1,0:T(2,128)(2,1)S(1)}, f32[1,2,56]{2,1,0:T(2,128)}, f32[1,2,56]{2,1,0:T(2,128)}, f32[1,2,56]{2,1,0:T(2,128)}) custom-call(f32[16,2,1152]{2,1,0:T(2,128)S(1)} %all_to_all.16.parts), custom_call_target="tpu_custom_call" | custom-call | tf_op jit(solution)/shard_map/pallas_call | solution.py:130
  61.6 18.5 %all_to_all.17.parts = bf16[64,2,896]{2,1,0:T(2,128)(2,1)S(1)} all-to-all(bf16[64,2,896]{2,1,0:T(2,128)(2,1)S(1)} %get-tuple-element.12), channel_id=1, replica_groups=mesh['zh'=4,'core'=2,'gy'=16,'gz'=8] {'zh','gy'}, dimensions={0} | all-to-all | bytes 458752 | tf_op jit(solution)/shard_map/all_to_all | solution.py:104
  80.1 0.8 %shard_map.96 = bf16[1,32,3584]{2,1,0:T(8,128)(2,1)} custom-call(bf16[64,2,896]{2,1,0:T(2,128)(2,1)S(1)} %all_to_all.17.parts), custom_call_target="tpu_custom_call" | custom-call | tf_op jit(solution)/shard_map/pallas_call | solution.py:139

commit v3 on v2

v3 whole, which is shorter than its diff:
```python
import functools

import jax
import jax.numpy as jnp
from jax import lax
from jax.experimental import pallas as pl
from jax.experimental.pallas import tpu as pltpu
from jax.sharding import Mesh, PartitionSpec as P

PLANE = ("core", "gy")
LINE = ("zh", "gz")
VMEM = pl.BlockSpec(memory_space=pltpu.VMEM)
SMEM = pl.BlockSpec(memory_space=pltpu.SMEM)
HBM = pl.BlockSpec(memory_space=pltpu.HBM)
PARAMS = pltpu.CompilerParams(vmem_limit_bytes=8 * 1024 * 1024)
F32, BF16 = jnp.float32, jnp.bfloat16


def accumulate(pieces, counts, tokens, grads, master, moment1, moment2, out, state, slots, acc, small, sems):
    _, n_slots, _, rows, width = grads.shape
    peers, _, block = out.shape
    n_rows = rows // 2
    cores, piece = peers // n_rows, block // pieces
    span = piece * cores
    copies = [
        pltpu.make_async_copy(grads.at[0, :, 0, :, pl.ds(z * span, span)], slots.at[:, :, pl.ds(z * span, span)], sems.at[z])
        for z in range(pieces)
    ]
    later = [pltpu.make_async_copy(x.at[0], small.at[i], sems.at[pieces + i]) for i, x in enumerate((master, moment1, moment2))]
    for copy in copies + later:
        copy.start()
    count = counts[0]
    weights = [(slot < count).astype(F32) for slot in range(n_slots)]
    for z in range(pieces):
        copies[z].wait()
        at = slice(z * span, (z + 1) * span)
        total = slots[0, :, at].astype(F32)
        for slot in range(1, n_slots):
            total = total + weights[slot] * slots[slot, :, at].astype(F32)
        for c in range(cores):
            acc[c, :, z * piece : (z + 1) * piece] = total[:, c * piece : (c + 1) * piece]
    for c in range(cores):
        for i in range(n_rows):
            out[c * n_rows + i] = acc[c, 2 * i : 2 * i + 2, :]
    for copy in later:
        copy.wait()
    w = small.shape[-1]
    for i in range(3):
        state[:, i * w : (i + 1) * w] = small[i]
    state[:, 3 * w :] = jnp.full((2, state.shape[1] - 3 * w), tokens[0].astype(F32))


def reduce_and_pack(parts, state, out):
    block = parts.shape[2]
    total = parts[0]
    for j in range(1, parts.shape[0]):
        total = total + parts[j]
    for j in range(out.shape[0]):
        out[j, :, :block] = total
        out[j, :, block:] = state[...]


def adam(parts, send, mine, state, result):
    peers = parts.shape[0]
    _, _, block = send.shape
    w = block // peers
    total = parts[0, :, :block]
    for j in range(1, peers):
        total = total + parts[j, :, :block]
    for j in range(peers):
        for i in range(3):
            state[i, :, j * w : (j + 1) * w] = parts[j, :, block + i * w : block + (i + 1) * w]
    master, moment1, moment2 = state[0], state[1], state[2]
    tokens = parts[0, 0:1, block + 3 * w : block + 3 * w + 1]
    gradient = total / tokens
    first = 0.9 * moment1 + 0.1 * gradient
    second = 0.95 * moment2 + 0.05 * gradient * gradient
    first_fix = 1.0 - 0.9**10
    second_fix = 1.0 - 0.95**10
    update = first / first_fix / (jnp.sqrt(second / second_fix) + 1e-08)
    new_master = master - 0.01 * (update + 0.1 * master)
    params = new_master.astype(BF16)
    for j in range(send.shape[0]):
        send[j] = params
    result[0], result[1], result[2] = new_master, first, second
    place = lax.axis_index(LINE)
    for j in range(peers):

        @pl.when(place == j)
        def _():
            for i in range(3):
                mine[i] = result[i, :, j * w : (j + 1) * w]


def assemble(pieces, parts, mine, params, master_out, moment1_out, moment2_out, whole, sems):
    peers, _, block = parts.shape
    rows, width = whole.shape
    n_rows = rows // 2
    cores, piece = peers // n_rows, block // pieces
    outs = [pltpu.make_async_copy(mine.at[i], x.at[0], sems.at[i]) for i, x in enumerate((master_out, moment1_out, moment2_out))]
    for copy in outs:
        copy.start()
    tile = 8
    for t in range(rows // tile):
        for i in range(t * tile // 2, (t + 1) * tile // 2):
            for c in range(cores):
                for z in range(pieces):
                    start = (z * cores + c) * piece
                    whole[2 * i : 2 * i + 2, start : start + piece] = parts[c * n_rows + i, :, z * piece : (z + 1) * piece]
        at = pl.ds(t * tile, tile)
        copy = pltpu.make_async_copy(whole.at[at], params.at[0, at], sems.at[3 + t])
        copy.start()
        outs.append(copy)
    for copy in outs:
        copy.wait()


def body(grads, counts, total_tokens, master, moment1, moment2):
    n_slots, _, rows, width = grads.shape[1:]
    n_plane, n_line = lax.axis_size(PLANE), lax.axis_size(LINE)
    block, w = rows * width // (2 * n_plane), master.shape[2]
    extra = -(-(3 * w + 1) // 128) * 128
    exchange = lambda x, axes: lax.all_to_all(x, axes, 0, 0, tiled=True)
    pieces = lax.axis_size("zh")
    pinned = [pltpu.with_memory_space_constraint(x, pltpu.HBM) for x in (grads, master, moment1, moment2)]

    parts, state = pl.pallas_call(
        functools.partial(accumulate, pieces),
        out_shape=(jax.ShapeDtypeStruct((n_plane, 2, block), F32), jax.ShapeDtypeStruct((2, extra), F32)),
        in_specs=[SMEM] * 2 + [HBM] * 4,
        out_specs=(VMEM, VMEM),
        scratch_shapes=[
            pltpu.VMEM((n_slots, rows, width), BF16),
            pltpu.VMEM((n_plane * 2 // rows, rows, block), F32),
            pltpu.VMEM((3, 2, w), F32),
            pltpu.SemaphoreType.DMA((pieces + 3,)),
        ],
        compiler_params=PARAMS,
    )(counts, total_tokens, *pinned)
    parts = exchange(parts, PLANE)
    packed = pl.pallas_call(
        reduce_and_pack,
        out_shape=jax.ShapeDtypeStruct((n_line, 2, block + extra), F32),
        in_specs=[VMEM, VMEM],
        out_specs=VMEM,
        compiler_params=PARAMS,
    )(parts, state)
    packed = exchange(packed, LINE)
    send, mine = pl.pallas_call(
        adam,
        out_shape=(jax.ShapeDtypeStruct((n_plane, 2, block), BF16), jax.ShapeDtypeStruct((3, 2, w), F32)),
        in_specs=[VMEM],
        out_specs=(VMEM, VMEM),
        scratch_shapes=[pltpu.VMEM((3, 2, block), F32), pltpu.VMEM((3, 2, block), F32)],
        compiler_params=PARAMS,
    )(packed)
    gathered = exchange(send, PLANE)
    shard = jax.ShapeDtypeStruct(master.shape, F32)
    return pl.pallas_call(
        functools.partial(assemble, pieces),
        out_shape=(jax.ShapeDtypeStruct((1, rows, width), BF16), shard, shard, shard),
        in_specs=[VMEM, VMEM],
        out_specs=(HBM,) * 4,
        scratch_shapes=[pltpu.VMEM((rows, width), BF16), pltpu.SemaphoreType.DMA((3 + rows // 8,))],
        compiler_params=PARAMS,
    )(gathered, mine)


def solution(mesh):
    gx, gy, gz = mesh.devices.shape
    fine = Mesh(mesh.devices.reshape(gx // 2, 2, gy, gz), ("zh", "core", "gy", "gz"))
    ranks = ("zh", "core", "gy", "gz")
    state = P(None, "gy", ("zh", "core", "gz"))
    return jax.shard_map(
        body,
        mesh=fine,
        in_specs=(P(ranks, None, None, None, None), P(ranks), P(), state, state, state),
        out_specs=(P(), state, state, state),
        check_vma=False,
    )
```

time: 81.1 us -> 87.1 us (1.074)
  blocking collectives: 75.7 us -> 82 us
    all_to_all x3, blocking collectives: 75.7 us -> 82 us  [body(): exchange = lambda x, axes: lax.all_to_all(x, axes, 0, 0, tiled=True)]
where the time goes in v3:
time: 87.1 us; the launch traced here: 86.9 us
  blocking collectives  82 us (94%)
  Pallas kernels  2.93 us (3%)
  between operations  1.95 us (2%)
    all_to_all x3, blocking collectives, body(): exchange = lambda x, axes: lax.all_to_all(x, axes, 0, 0, tiled=True)  82 us

profile of v3, /device:TPU:2, one launch (start us, length us, event | category | flops | bytes accessed | tf_op | source)
XLA Modules:
  0.0 86.9 jit_solution(15189294515490420637)
XLA Ops:
  1.9 1.6 %shard_map.93 = (f32[32,2,1792]{2,1,0:T(2,128)S(1)}, f32[2,256]{1,0:T(2,128)S(1)}) custom-call(s32[1]{0:T(128)S(6)} %copy.10.counts, s32[1]{0:T(128)S(6)} %copy.11.tokens, bf16[1,4,1,32,3584]{4,3,2,1,0:T(8,128)(2,1)} %grads.1, f32[1,2,56]{2,1,0:T(2,128)} %master.1, f32[1,2,56]{2,1,0:T(2,128)} %moment1.1, f32[1,2,56]{2,1,0:T(2,128)} %moment2.1), custom_call_target="tpu_custom_call" | custom-call | tf_op jit(solution)/shard_map/pallas_call | solution.py:127
  3.5 25.5 %all_to_all.15.parts = f32[32,2,1792]{2,1,0:T(2,128)S(1)} all-to-all(f32[32,2,1792]{2,1,0:T(2,128)S(1)} %get-tuple-element.8), channel_id=1, replica_groups=mesh['zh'=4,'core'=2,'gy'=16,'gz'=8] {'core','gy'}, dimensions={0} | all-to-all | bytes 917504 | tf_op jit(solution)/shard_map/all_to_all | solution.py:123
  29.0 0.1 shard_map.94
  29.1 40.2 %all_to_all.16.parts = f32[32,2,2048]{2,1,0:T(2,128)S(1)} all-to-all(f32[32,2,2048]{2,1,0:T(2,128)S(1)} %shard_map.94), channel_id=1, replica_groups=mesh['zh'=4,'core'=2,'gy'=16,'gz'=8] {'zh','gz'}, dimensions={0} | all-to-all | bytes 1048576 | tf_op jit(solution)/shard_map/all_to_all | solution.py:123
  69.3 0.4 shard_map.95
  69.7 16.2 %all_to_all.17.parts = bf16[32,2,1792]{2,1,0:T(2,128)(2,1)S(1)} all-to-all(bf16[32,2,1792]{2,1,0:T(2,128)(2,1)S(1)} %get-tuple-element.10), channel_id=1, replica_groups=mesh['zh'=4,'core'=2,'gy'=16,'gz'=8] {'core','gy'}, dimensions={0} | all-to-all | bytes 458752 | tf_op jit(solution)/shard_map/all_to_all | solution.py:123
  86.0 0.9 %shard_map.96 = (bf16[1,32,3584]{2,1,0:T(8,128)(2,1)}, f32[1,2,56]{2,1,0:T(2,128)}, f32[1,2,56]{2,1,0:T(2,128)}, f32[1,2,56]{2,1,0:T(2,128)}) custom-call(bf16[32,2,1792]{2,1,0:T(2,128)(2,1)S(1)} %all_to_all.17.parts, f32[3,2,56]{2,1,0:T(2,128)S(1)} %get-tuple-element.11.mine), custom_call_target="tpu_custom_call" | custom-call | tf_op jit(solution)/shard_map/pallas_call | solution.py:159

commit v4 on v3

--- a/solution.py
+++ b/solution.py
@@ -1,5 +1,3 @@
-import functools
-
 import jax
 import jax.numpy as jnp
 from jax import lax
@@ -7,8 +5,8 @@
 from jax.experimental.pallas import tpu as pltpu
 from jax.sharding import Mesh, PartitionSpec as P
 
-PLANE = ("core", "gy")
-LINE = ("zh", "gz")
+PLANE = ("gy", "zh")
+LINE = ("core", "gz")
 VMEM = pl.BlockSpec(memory_space=pltpu.VMEM)
 SMEM = pl.BlockSpec(memory_space=pltpu.SMEM)
 HBM = pl.BlockSpec(memory_space=pltpu.HBM)
@@ -16,32 +14,28 @@
 F32, BF16 = jnp.float32, jnp.bfloat16
 
 
-def accumulate(pieces, counts, tokens, grads, master, moment1, moment2, out, state, slots, acc, small, sems):
+def accumulate(counts, tokens, grads, master, moment1, moment2, out, state, slots, acc, small, sems):
     _, n_slots, _, rows, width = grads.shape
-    peers, _, block = out.shape
-    n_rows = rows // 2
-    cores, piece = peers // n_rows, block // pieces
-    span = piece * cores
+    _, _, block = out.shape
+    spans = width // block
     copies = [
-        pltpu.make_async_copy(grads.at[0, :, 0, :, pl.ds(z * span, span)], slots.at[:, :, pl.ds(z * span, span)], sems.at[z])
-        for z in range(pieces)
+        pltpu.make_async_copy(grads.at[0, :, 0, :, pl.ds(z * block, block)], slots.at[:, :, pl.ds(z * block, block)], sems.at[z])
+        for z in range(spans)
     ]
-    later = [pltpu.make_async_copy(x.at[0], small.at[i], sems.at[pieces + i]) for i, x in enumerate((master, moment1, moment2))]
+    later = [pltpu.make_async_copy(x.at[0], small.at[i], sems.at[spans + i]) for i, x in enumerate((master, moment1, moment2))]
     for copy in copies + later:
         copy.start()
     count = counts[0]
     weights = [(slot < count).astype(F32) for slot in range(n_slots)]
-    for z in range(pieces):
+    for z in range(spans):
         copies[z].wait()
-        at = slice(z * span, (z + 1) * span)
+        at = slice(z * block, (z + 1) * block)
         total = slots[0, :, at].astype(F32)
         for slot in range(1, n_slots):
             total = total + weights[slot] * slots[slot, :, at].astype(F32)
-        for c in range(cores):
-            acc[c, :, z * piece : (z + 1) * piece] = total[:, c * piece : (c + 1) * piece]
-    for c in range(cores):
-        for i in range(n_rows):
-            out[c * n_rows + i] = acc[c, 2 * i : 2 * i + 2, :]
+        acc[:, at] = total
+        for i in range(rows // 2):
+            out[i * spans + z] = acc[2 * i : 2 * i + 2, at]
     for copy in later:
         copy.wait()
     w = small.shape[-1]
@@ -92,22 +86,18 @@
                 mine[i] = result[i, :, j * w : (j + 1) * w]
 
 
-def assemble(pieces, parts, mine, params, master_out, moment1_out, moment2_out, whole, sems):
-    peers, _, block = parts.shape
+def assemble(parts, mine, params, master_out, moment1_out, moment2_out, whole, sems):
+    _, _, block = parts.shape
     rows, width = whole.shape
-    n_rows = rows // 2
-    cores, piece = peers // n_rows, block // pieces
+    spans = width // block
     outs = [pltpu.make_async_copy(mine.at[i], x.at[0], sems.at[i]) for i, x in enumerate((master_out, moment1_out, moment2_out))]
     for copy in outs:
         copy.start()
-    tile = 8
-    for t in range(rows // tile):
-        for i in range(t * tile // 2, (t + 1) * tile // 2):
-            for c in range(cores):
-                for z in range(pieces):
-                    start = (z * cores + c) * piece
-                    whole[2 * i : 2 * i + 2, start : start + piece] = parts[c * n_rows + i, :, z * piece : (z + 1) * piece]
-        at = pl.ds(t * tile, tile)
+    for t in range(rows // 8):
+        for i in range(4 * t, 4 * t + 4):
+            for z in range(spans):
+                whole[2 * i : 2 * i + 2, z * block : (z + 1) * block] = parts[i * spans + z]
+        at = pl.ds(8 * t, 8)
         copy = pltpu.make_async_copy(whole.at[at], params.at[0, at], sems.at[3 + t])
         copy.start()
         outs.append(copy)
@@ -121,19 +111,18 @@
     block, w = rows * width // (2 * n_plane), master.shape[2]
     extra = -(-(3 * w + 1) // 128) * 128
     exchange = lambda x, axes: lax.all_to_all(x, axes, 0, 0, tiled=True)
-    pieces = lax.axis_size("zh")
     pinned = [pltpu.with_memory_space_constraint(x, pltpu.HBM) for x in (grads, master, moment1, moment2)]
 
     parts, state = pl.pallas_call(
-        functools.partial(accumulate, pieces),
+        accumulate,
         out_shape=(jax.ShapeDtypeStruct((n_plane, 2, block), F32), jax.ShapeDtypeStruct((2, extra), F32)),
         in_specs=[SMEM] * 2 + [HBM] * 4,
         out_specs=(VMEM, VMEM),
         scratch_shapes=[
             pltpu.VMEM((n_slots, rows, width), BF16),
-            pltpu.VMEM((n_plane * 2 // rows, rows, block), F32),
+            pltpu.VMEM((rows, width), F32),
             pltpu.VMEM((3, 2, w), F32),
-            pltpu.SemaphoreType.DMA((pieces + 3,)),
+            pltpu.SemaphoreType.DMA((width // block + 3,)),
         ],
         compiler_params=PARAMS,
     )(counts, total_tokens, *pinned)
@@ -157,7 +146,7 @@
     gathered = exchange(send, PLANE)
     shard = jax.ShapeDtypeStruct(master.shape, F32)
     return pl.pallas_call(
-        functools.partial(assemble, pieces),
+        assemble,
         out_shape=(jax.ShapeDtypeStruct((1, rows, width), BF16), shard, shard, shard),
         in_specs=[VMEM, VMEM],
         out_specs=(HBM,) * 4,

time: 87.1 us -> 79.6 us (0.914)
  blocking collectives: 82 us -> 74.8 us
    all_to_all x3, blocking collectives: 82 us -> 74.8 us  [body(): exchange = lambda x, axes: lax.all_to_all(x, axes, 0, 0, tiled=True)]
where the time goes in v4:
time: 79.6 us; the launch traced here: 79.4 us
  blocking collectives  74.8 us (94%)
  Pallas kernels  2.63 us (3%)
  between operations  1.94 us (2%)
    all_to_all x3, blocking collectives, body(): exchange = lambda x, axes: lax.all_to_all(x, axes, 0, 0, tiled=True)  74.8 us

profile of v4, /device:TPU:2, one launch (start us, length us, event | category | flops | bytes accessed | tf_op | source)
XLA Modules:
  0.0 79.4 jit_solution(929792237894689720)
XLA Ops:
  1.9 1.5 %shard_map.93 = (f32[64,2,896]{2,1,0:T(2,128)S(1)}, f32[2,256]{1,0:T(2,128)S(1)}) custom-call(s32[1]{0:T(128)S(6)} %copy.10.counts, s32[1]{0:T(128)S(6)} %copy.11.tokens, bf16[1,4,1,32,3584]{4,3,2,1,0:T(8,128)(2,1)} %grads.1, f32[1,2,56]{2,1,0:T(2,128)} %master.1, f32[1,2,56]{2,1,0:T(2,128)} %moment1.1, f32[1,2,56]{2,1,0:T(2,128)} %moment2.1), custom_call_target="tpu_custom_call" | custom-call | tf_op jit(solution)/shard_map/pallas_call | solution.py:116
  3.4 40.3 %all_to_all.15.parts = f32[64,2,896]{2,1,0:T(2,128)S(1)} all-to-all(f32[64,2,896]{2,1,0:T(2,128)S(1)} %get-tuple-element.8), channel_id=1, replica_groups=mesh['zh'=4,'core'=2,'gy'=16,'gz'=8] {'gy','zh'}, dimensions={0} | all-to-all | bytes 917504 | tf_op jit(solution)/shard_map/all_to_all | solution.py:113
  43.7 0.1 shard_map.94
  43.8 15.6 %all_to_all.16.parts = f32[16,2,1152]{2,1,0:T(2,128)S(1)} all-to-all(f32[16,2,1152]{2,1,0:T(2,128)S(1)} %shard_map.94), channel_id=1, replica_groups=mesh['zh'=4,'core'=2,'gy'=16,'gz'=8] {'core','gz'}, dimensions={0} | all-to-all | bytes 294912 | tf_op jit(solution)/shard_map/all_to_all | solution.py:113
  59.4 0.2 shard_map.95
  59.6 18.9 %all_to_all.17.parts = bf16[64,2,896]{2,1,0:T(2,128)(2,1)S(1)} all-to-all(bf16[64,2,896]{2,1,0:T(2,128)(2,1)S(1)} %get-tuple-element.10), channel_id=1, replica_groups=mesh['zh'=4,'core'=2,'gy'=16,'gz'=8] {'gy','zh'}, dimensions={0} | all-to-all | bytes 458752 | tf_op jit(solution)/shard_map/all_to_all | solution.py:113
  78.5 0.8 %shard_map.96 = (bf16[1,32,3584]{2,1,0:T(8,128)(2,1)}, f32[1,2,56]{2,1,0:T(2,128)}, f32[1,2,56]{2,1,0:T(2,128)}, f32[1,2,56]{2,1,0:T(2,128)}) custom-call(bf16[64,2,896]{2,1,0:T(2,128)(2,1)S(1)} %all_to_all.17.parts, f32[3,2,56]{2,1,0:T(2,128)S(1)} %get-tuple-element.11.mine), custom_call_target="tpu_custom_call" | custom-call | tf_op jit(solution)/shard_map/pallas_call | solution.py:148

commit v5 on v4

--- a/solution.py
+++ b/solution.py
@@ -14,58 +14,77 @@
 F32, BF16 = jnp.float32, jnp.bfloat16
 
 
-def accumulate(counts, tokens, grads, master, moment1, moment2, out, state, slots, acc, small, sems):
+def accumulate(counts, grads, master, moment1, moment2, keep, give, state, slots, acc, small, sems):
     _, n_slots, _, rows, width = grads.shape
-    _, _, block = out.shape
-    spans = width // block
+    half = keep.shape[2]
+    spans, span = width // (2 * half), 2 * half
     copies = [
-        pltpu.make_async_copy(grads.at[0, :, 0, :, pl.ds(z * block, block)], slots.at[:, :, pl.ds(z * block, block)], sems.at[z])
+        pltpu.make_async_copy(grads.at[0, :, 0, :, pl.ds(z * span, span)], slots.at[:, :, pl.ds(z * span, span)], sems.at[z])
         for z in range(spans)
     ]
     later = [pltpu.make_async_copy(x.at[0], small.at[i], sems.at[spans + i]) for i, x in enumerate((master, moment1, moment2))]
     for copy in copies + later:
         copy.start()
+    core = lax.axis_index("core")
     count = counts[0]
     weights = [(slot < count).astype(F32) for slot in range(n_slots)]
     for z in range(spans):
         copies[z].wait()
-        at = slice(z * block, (z + 1) * block)
+        at = slice(z * span, (z + 1) * span)
         total = slots[0, :, at].astype(F32)
         for slot in range(1, n_slots):
             total = total + weights[slot] * slots[slot, :, at].astype(F32)
-        acc[:, at] = total
-        for i in range(rows // 2):
-            out[i * spans + z] = acc[2 * i : 2 * i + 2, at]
+        acc[0, :, z * half : (z + 1) * half] = total[:, :half]
+        acc[1, :, z * half : (z + 1) * half] = total[:, half:]
+    for own in range(2):
+
+        @pl.when(core == own)
+        def _():
+            for c, out in ((own, keep), (1 - own, give)):
+                for i in range(rows // 2):
+                    for z in range(spans):
+                        out[i * spans + z] = acc[c, 2 * i : 2 * i + 2, z * half : (z + 1) * half]
+
     for copy in later:
         copy.wait()
     w = small.shape[-1]
     for i in range(3):
         state[:, i * w : (i + 1) * w] = small[i]
-    state[:, 3 * w :] = jnp.full((2, state.shape[1] - 3 * w), tokens[0].astype(F32))
+
+
+def add(tokens, x, y, shards, out, state):
+    used, extra = shards.shape[1], state.shape[1]
+    out[...] = x[...] + y[...]
+    state[:, :used] = shards[...]
+    state[:, used:] = jnp.full((2, extra - used), tokens[0].astype(F32))
 
 
 def reduce_and_pack(parts, state, out):
-    block = parts.shape[2]
+    half = parts.shape[2]
+    extra = out.shape[2] - half
     total = parts[0]
     for j in range(1, parts.shape[0]):
         total = total + parts[j]
     for j in range(out.shape[0]):
-        out[j, :, :block] = total
-        out[j, :, block:] = state[...]
+        out[j, :, :half] = total
+        out[j, :, half:] = state[:, :extra]
 
 
-def adam(parts, send, mine, state, result):
+def adam(parts, send, mine, summed, state, result):
     peers = parts.shape[0]
     _, _, block = send.shape
-    w = block // peers
-    total = parts[0, :, :block]
-    for j in range(1, peers):
-        total = total + parts[j, :, :block]
+    w, half = block // peers, block // 2
+    for c in range(2):
+        total = parts[c * peers // 2, :, :half]
+        for j in range(c * peers // 2 + 1, (c + 1) * peers // 2):
+            total = total + parts[j, :, :half]
+        summed[:, c * half : (c + 1) * half] = total
+    total = summed[...]
     for j in range(peers):
         for i in range(3):
-            state[i, :, j * w : (j + 1) * w] = parts[j, :, block + i * w : block + (i + 1) * w]
+            state[i, :, j * w : (j + 1) * w] = parts[j, :, half + i * w : half + (i + 1) * w]
     master, moment1, moment2 = state[0], state[1], state[2]
-    tokens = parts[0, 0:1, block + 3 * w : block + 3 * w + 1]
+    tokens = parts[0, 0:1, half + 3 * w : half + 3 * w + 1]
     gradient = total / tokens
     first = 0.9 * moment1 + 0.1 * gradient
     second = 0.95 * moment2 + 0.05 * gradient * gradient
@@ -109,27 +128,37 @@
     n_slots, _, rows, width = grads.shape[1:]
     n_plane, n_line = lax.axis_size(PLANE), lax.axis_size(LINE)
     block, w = rows * width // (2 * n_plane), master.shape[2]
-    extra = -(-(3 * w + 1) // 128) * 128
+    half = block // 2
+    whole = -(-(half + 3 * w + 1) // 128) * 128
     exchange = lambda x, axes: lax.all_to_all(x, axes, 0, 0, tiled=True)
     pinned = [pltpu.with_memory_space_constraint(x, pltpu.HBM) for x in (grads, master, moment1, moment2)]
 
-    parts, state = pl.pallas_call(
+    piece = jax.ShapeDtypeStruct((n_plane, 2, half), F32)
+    keep, give, shards = pl.pallas_call(
         accumulate,
-        out_shape=(jax.ShapeDtypeStruct((n_plane, 2, block), F32), jax.ShapeDtypeStruct((2, extra), F32)),
-        in_specs=[SMEM] * 2 + [HBM] * 4,
-        out_specs=(VMEM, VMEM),
+        out_shape=(piece, piece, jax.ShapeDtypeStruct((2, 3 * w), F32)),
+        in_specs=[SMEM] + [HBM] * 4,
+        out_specs=(VMEM,) * 3,
         scratch_shapes=[
             pltpu.VMEM((n_slots, rows, width), BF16),
-            pltpu.VMEM((rows, width), F32),
+            pltpu.VMEM((2, rows, width // 2), F32),
             pltpu.VMEM((3, 2, w), F32),
             pltpu.SemaphoreType.DMA((width // block + 3,)),
         ],
         compiler_params=PARAMS,
-    )(counts, total_tokens, *pinned)
+    )(counts, *pinned)
+    given = lax.ppermute(give, "core", [(0, 1), (1, 0)])
+    parts, state = pl.pallas_call(
+        add,
+        out_shape=(piece, jax.ShapeDtypeStruct((2, whole - half), F32)),
+        in_specs=[SMEM] + [VMEM] * 3,
+        out_specs=(VMEM, VMEM),
+        compiler_params=PARAMS,
+    )(total_tokens, keep, given, shards)
     parts = exchange(parts, PLANE)
     packed = pl.pallas_call(
         reduce_and_pack,
-        out_shape=jax.ShapeDtypeStruct((n_line, 2, block + extra), F32),
+        out_shape=jax.ShapeDtypeStruct((n_line, 2, whole), F32),
         in_specs=[VMEM, VMEM],
         out_specs=VMEM,
         compiler_params=PARAMS,
@@ -140,7 +169,7 @@
         out_shape=(jax.ShapeDtypeStruct((n_plane, 2, block), BF16), jax.ShapeDtypeStruct((3, 2, w), F32)),
         in_specs=[VMEM],
         out_specs=(VMEM, VMEM),
-        scratch_shapes=[pltpu.VMEM((3, 2, block), F32), pltpu.VMEM((3, 2, block), F32)],
+        scratch_shapes=[pltpu.VMEM((2, block), F32), pltpu.VMEM((3, 2, block), F32), pltpu.VMEM((3, 2, block), F32)],
         compiler_params=PARAMS,
     )(packed)
     gathered = exchange(send, PLANE)

time: 79.6 us -> 77.7 us (0.976)
  blocking collectives: 74.8 us -> 69.8 us
  starting transfers between devices: 0 us -> 1.92 us
  waiting for transfers between devices: 0 us -> 0.85 us
    all_to_all x3, blocking collectives: 74.8 us -> 69.8 us  [body(): exchange = lambda x, axes: lax.all_to_all(x, axes, 0, 0, tiled=True)]
    ppermute x0 -> x1, starting transfers between devices: none -> 1.92 us  [body(): given = lax.ppermute(give, 'core', [(0, 1), (1, 0)])]
    ppermute x0 -> x1, waiting for transfers between devices: none -> 0.85 us  [body(): given = lax.ppermute(give, 'core', [(0, 1), (1, 0)])]
    pallas_call x1 -> x2, Pallas kernels: 1.49 us -> 1.7 us  [the longest x1 1.67 us: body(): pl.pallas_call(accumulate, out_shape=(piece, piece, jax.ShapeDtypeStruct(...]
  transfers between devices with their start and end apart: 0 -> 1, of which waited for: 0 -> 1; matrix products, arithmetic and copies ran while one was open for 0% -> 0% of each run, Pallas kernels for 0% -> 0%
where the time goes in v5:
time: 77.7 us; the launch traced here: 77.4 us
  blocking collectives  69.8 us (90%)
  Pallas kernels  2.85 us (4%)
  between operations  1.95 us (3%)
  starting transfers between devices  1.92 us (2%)
  waiting for transfers between devices  0.85 us (1%)
    all_to_all x3, blocking collectives, body(): exchange = lambda x, axes: lax.all_to_all(x, axes, 0, 0, tiled=True)  69.8 us
    ppermute x1, starting transfers between devices, body(): given = lax.ppermute(give, 'core', [(0, 1), (1, 0)])  1.92 us
    pallas_call x1, Pallas kernels, body(): pl.pallas_call(accumulate, out_shape=(piece, piece, jax.ShapeDtypeStruct(...  1.67 us
  transfers between devices with their start and end apart: 1, of which 1 were waited for; matrix products, arithmetic and copies ran while one was open for 0% of the time, Pallas kernels for 0%

profile of v5, /device:TPU:2, one launch (start us, length us, event | category | flops | bytes accessed | tf_op | source)
XLA Modules:
  0.0 77.4 jit_solution(8171208691827757100)
XLA Ops:
  1.3 1.7 %shard_map.93 = (f32[64,2,448]{2,1,0:T(2,128)S(1)}, f32[64,2,448]{2,1,0:T(2,128)S(1)}, f32[2,168]{1,0:T(2,128)S(1)}) custom-call(s32[1]{0:T(128)S(6)} %copy.10.counts, bf16[1,4,1,32,3584]{4,3,2,1,0:T(8,128)(2,1)} %grads.1, f32[1,2,56]{2,1,0:T(2,128)} %master.1, f32[1,2,56]{2,1,0:T(2,128)} %moment1.1, f32[1,2,56]{2,1,0:T(2,128)} %moment2.1), custom_call_target="tpu_custom_call" | custom-call | tf_op jit(solution)/shard_map/pallas_call | solution.py:137
  2.9 1.9 %collective-permute-start = (f32[64,2,448]{2,1,0:T(2,128)S(1)}, f32[64,2,448]{2,1,0:T(2,128)S(1)}, u32[]{:S(2)}, u32[]{:S(2)}) collective-permute-start(f32[64,2,448]{2,1,0:T(2,128)S(1)} %get-tuple-element.12), channel_id=1, source_target_pairs={{0,128},{128,0},{1,129},{129,1},{2,130},{130,2},{3,131},{131,3},{4... | collective-permute-start | bytes 688136 | tf_op jit(solution)/shard_map/ppermute | solution.py:150
  5.5 0.9 %collective-permute-done.y = f32[64,2,448]{2,1,0:T(2,128)S(1)} collective-permute-done((f32[64,2,448]{2,1,0:T(2,128)S(1)}, f32[64,2,448]{2,1,0:T(2,128)S(1)}, u32[]{:S(2)}, u32[]{:S(2)}) %collective-permute-start) | collective-permute-done | bytes 229408 | tf_op jit(solution)/shard_map/ppermute | solution.py:150
  6.4 37.4 %all_to_all.15.parts = f32[64,2,448]{2,1,0:T(2,128)S(1)} all-to-all(f32[64,2,448]{2,1,0:T(2,128)S(1)} %get-tuple-element.14), channel_id=1, replica_groups=mesh['zh'=4,'core'=2,'gy'=16,'gz'=8] {'gy','zh'}, dimensions={0} | all-to-all | bytes 458752 | tf_op jit(solution)/shard_map/all_to_all | solution.py:133
  43.8 0.1 shard_map.95
  43.9 14.4 %all_to_all.16.parts = f32[16,2,640]{2,1,0:T(2,128)S(1)} all-to-all(f32[16,2,640]{2,1,0:T(2,128)S(1)} %shard_map.95), channel_id=1, replica_groups=mesh['zh'=4,'core'=2,'gy'=16,'gz'=8] {'core','gz'}, dimensions={0} | all-to-all | bytes 163840 | tf_op jit(solution)/shard_map/all_to_all | solution.py:133
  58.2 0.2 shard_map.96
  58.5 18.1 %all_to_all.17.parts = bf16[64,2,896]{2,1,0:T(2,128)(2,1)S(1)} all-to-all(bf16[64,2,896]{2,1,0:T(2,128)(2,1)S(1)} %get-tuple-element.16), channel_id=1, replica_groups=mesh['zh'=4,'core'=2,'gy'=16,'gz'=8] {'gy','zh'}, dimensions={0} | all-to-all | bytes 458752 | tf_op jit(solution)/shard_map/all_to_all | solution.py:133
  76.6 0.8 %shard_map.97 = (bf16[1,32,3584]{2,1,0:T(8,128)(2,1)}, f32[1,2,56]{2,1,0:T(2,128)}, f32[1,2,56]{2,1,0:T(2,128)}, f32[1,2,56]{2,1,0:T(2,128)}) custom-call(bf16[64,2,896]{2,1,0:T(2,128)(2,1)S(1)} %all_to_all.17.parts, f32[3,2,56]{2,1,0:T(2,128)S(1)} %get-tuple-element.17.mine), custom_call_target="tpu_custom_call" | custom-call | tf_op jit(solution)/shard_map/pallas_call | solution.py:177
  (1 shorter events, 0.0 us)
Async XLA Ops:
  2.9 3.4 %collective-permute-start = (f32[64,2,448]{2,1,0:T(2,128)S(1)}, f32[64,2,448]{2,1,0:T(2,128)S(1)}, u32[]{:S(2)}, u32[]{:S(2)}) collective-permute-start(f32[64,2,448]{2,1,0:T(2,128)S(1)} %get-tuple-element.12), channel_id=1, source_target_pairs={{0,128},{128,0},{1,129},{129,1},{2,130},{130,2},{3,131},{131,3},{4... | collective-permute-start | bytes 688136 | tf_op jit(solution)/shard_map/ppermute | solution.py:150

commit v6 on v5

--- a/solution.py
+++ b/solution.py
@@ -11,13 +11,14 @@
 SMEM = pl.BlockSpec(memory_space=pltpu.SMEM)
 HBM = pl.BlockSpec(memory_space=pltpu.HBM)
 PARAMS = pltpu.CompilerParams(vmem_limit_bytes=8 * 1024 * 1024)
+LANES, TILE, PAIRS = 128, 8, 6
 F32, BF16 = jnp.float32, jnp.bfloat16
 
 
-def accumulate(counts, grads, master, moment1, moment2, keep, give, state, slots, acc, small, sems):
+def accumulate(counts, grads, master, moment1, moment2, keep, give, shards, slots, acc, small, sems):
     _, n_slots, _, rows, width = grads.shape
-    half = keep.shape[2]
-    spans, span = width // (2 * half), 2 * half
+    spans = 2 * keep.shape[0] // (TILE * rows)
+    span, lines = width // spans, width // (spans * LANES)
     copies = [
         pltpu.make_async_copy(grads.at[0, :, 0, :, pl.ds(z * span, span)], slots.at[:, :, pl.ds(z * span, span)], sems.at[z])
         for z in range(spans)
@@ -28,63 +29,66 @@
     core = lax.axis_index("core")
     count = counts[0]
     weights = [(slot < count).astype(F32) for slot in range(n_slots)]
+    group = min(TILE, rows // 2)
     for z in range(spans):
         copies[z].wait()
         at = slice(z * span, (z + 1) * span)
         total = slots[0, :, at].astype(F32)
         for slot in range(1, n_slots):
             total = total + weights[slot] * slots[slot, :, at].astype(F32)
-        acc[0, :, z * half : (z + 1) * half] = total[:, :half]
-        acc[1, :, z * half : (z + 1) * half] = total[:, half:]
-    for own in range(2):
-
-        @pl.when(core == own)
-        def _():
-            for c, out in ((own, keep), (1 - own, give)):
-                for i in range(rows // 2):
-                    for z in range(spans):
-                        out[i * spans + z] = acc[c, 2 * i : 2 * i + 2, z * half : (z + 1) * half]
-
+        for k in range(lines):
+            acc[z * lines + k] = total[:, k * LANES : (k + 1) * LANES]
+        for k in range(lines):
+            for i in range(0, rows // 2, group):
+                to = pl.ds((i * spans + z) * TILE + k, group, stride=spans * TILE)
+                keep[to, :] = acc[z * lines + k, pl.ds(2 * i + core, group, stride=2), :]
+                give[to, :] = acc[z * lines + k, pl.ds(2 * i + 1 - core, group, stride=2), :]
     for copy in later:
         copy.wait()
     w = small.shape[-1]
-    for i in range(3):
-        state[:, i * w : (i + 1) * w] = small[i]
+    shards[...] = jnp.zeros(shards.shape, F32)
+    shards[0, :, :w] = small[0]
+    shards[0, :, w : 2 * w] = small[1]
+    shards[1, :, :w] = small[2]
 
 
 def add(tokens, x, y, shards, out, state):
-    used, extra = shards.shape[1], state.shape[1]
     out[...] = x[...] + y[...]
-    state[:, :used] = shards[...]
-    state[:, used:] = jnp.full((2, extra - used), tokens[0].astype(F32))
+    state[...] = shards[...]
+    state[1, :, LANES - 1 :] = jnp.full((2, 1), tokens[0].astype(F32))
 
 
 def reduce_and_pack(parts, state, out):
-    half = parts.shape[2]
-    extra = out.shape[2] - half
-    total = parts[0]
-    for j in range(1, parts.shape[0]):
-        total = total + parts[j]
-    for j in range(out.shape[0]):
-        out[j, :, :half] = total
-        out[j, :, half:] = state[:, :extra]
+    total = parts[0:TILE, :]
+    for j in range(TILE, parts.shape[0], TILE):
+        total = total + parts[j : j + TILE, :]
+    for j in range(0, out.shape[0], PAIRS):
+        for r in range(PAIRS - 2):
+            out[j + r] = total[2 * r : 2 * r + 2, :]
+        out[j + PAIRS - 2] = state[0]
+        out[j + PAIRS - 1] = state[1]
 
 
 def adam(parts, send, mine, summed, state, result):
-    peers = parts.shape[0]
+    peers = parts.shape[0] // PAIRS
     _, _, block = send.shape
-    w, half = block // peers, block // 2
+    w = block // peers
     for c in range(2):
-        total = parts[c * peers // 2, :, :half]
-        for j in range(c * peers // 2 + 1, (c + 1) * peers // 2):
-            total = total + parts[j, :, :half]
-        summed[:, c * half : (c + 1) * half] = total
+        for r in range(-(-block // (2 * LANES))):
+            first = c * peers // 2
+            total = parts[first * PAIRS + r]
+            for j in range(first + 1, first + peers // 2):
+                total = total + parts[j * PAIRS + r]
+            for k in range(2 * r, min(2 * r + 2, block // LANES)):
+                summed[c : c + 1, k * LANES : (k + 1) * LANES] = total[k - 2 * r : k - 2 * r + 1, :]
     total = summed[...]
     for j in range(peers):
-        for i in range(3):
-            state[i, :, j * w : (j + 1) * w] = parts[j, :, half + i * w : half + (i + 1) * w]
+        at = slice(j * w, (j + 1) * w)
+        state[0, :, at] = parts[j * PAIRS + PAIRS - 2, :, :w]
+        state[1, :, at] = parts[j * PAIRS + PAIRS - 2, :, w : 2 * w]
+        state[2, :, at] = parts[j * PAIRS + PAIRS - 1, :, :w]
     master, moment1, moment2 = state[0], state[1], state[2]
-    tokens = parts[0, 0:1, half + 3 * w : half + 3 * w + 1]
+    tokens = parts[PAIRS - 1, 0:1, LANES - 1 :]
     gradient = total / tokens
     first = 0.9 * moment1 + 0.1 * gradient
     second = 0.95 * moment2 + 0.05 * gradient * gradient
@@ -128,20 +132,19 @@
     n_slots, _, rows, width = grads.shape[1:]
     n_plane, n_line = lax.axis_size(PLANE), lax.axis_size(LINE)
     block, w = rows * width // (2 * n_plane), master.shape[2]
-    half = block // 2
-    whole = -(-(half + 3 * w + 1) // 128) * 128
     exchange = lambda x, axes: lax.all_to_all(x, axes, 0, 0, tiled=True)
     pinned = [pltpu.with_memory_space_constraint(x, pltpu.HBM) for x in (grads, master, moment1, moment2)]
 
-    piece = jax.ShapeDtypeStruct((n_plane, 2, half), F32)
+    tiles = jax.ShapeDtypeStruct((n_plane * TILE, LANES), F32)
+    pairs = jax.ShapeDtypeStruct((2, 2, LANES), F32)
     keep, give, shards = pl.pallas_call(
         accumulate,
-        out_shape=(piece, piece, jax.ShapeDtypeStruct((2, 3 * w), F32)),
+        out_shape=(tiles, tiles, pairs),
         in_specs=[SMEM] + [HBM] * 4,
         out_specs=(VMEM,) * 3,
         scratch_shapes=[
             pltpu.VMEM((n_slots, rows, width), BF16),
-            pltpu.VMEM((2, rows, width // 2), F32),
+            pltpu.VMEM((width // LANES, rows, LANES), F32),
             pltpu.VMEM((3, 2, w), F32),
             pltpu.SemaphoreType.DMA((width // block + 3,)),
         ],
@@ -150,7 +153,7 @@
     given = lax.ppermute(give, "core", [(0, 1), (1, 0)])
     parts, state = pl.pallas_call(
         add,
-        out_shape=(piece, jax.ShapeDtypeStruct((2, whole - half), F32)),
+        out_shape=(tiles, pairs),
         in_specs=[SMEM] + [VMEM] * 3,
         out_specs=(VMEM, VMEM),
         compiler_params=PARAMS,
@@ -158,7 +161,7 @@
     parts = exchange(parts, PLANE)
     packed = pl.pallas_call(
         reduce_and_pack,
-        out_shape=jax.ShapeDtypeStruct((n_line, 2, whole), F32),
+        out_shape=jax.ShapeDtypeStruct((n_line * PAIRS, 2, LANES), F32),
         in_specs=[VMEM, VMEM],
         out_specs=VMEM,
         compiler_params=PARAMS,

time: 77.7 us -> 77.8 us (level)
  no operation moved by 1% of the time
where the time goes in v6:
time: 77.8 us; the launch traced here: 77.5 us
  blocking collectives  70 us (90%)
  Pallas kernels  2.75 us (4%)
  between operations  1.95 us (3%)
  starting transfers between devices  1.92 us (2%)
  waiting for transfers between devices  0.85 us (1%)
    all_to_all x3, blocking collectives, body(): exchange = lambda x, axes: lax.all_to_all(x, axes, 0, 0, tiled=True)  70 us
    ppermute x1, starting transfers between devices, body(): given = lax.ppermute(give, 'core', [(0, 1), (1, 0)])  1.92 us
    pallas_call x1, Pallas kernels, body(): pl.pallas_call(accumulate, out_shape=(tiles, tiles, pairs), in_specs=[SME...  1.59 us
  transfers between devices with their start and end apart: 1, of which 1 were waited for; matrix products, arithmetic and copies ran while one was open for 0% of the time, Pallas kernels for 0%

profile of v6, /device:TPU:2, one launch (start us, length us, event | category | flops | bytes accessed | tf_op | source)
XLA Modules:
  0.0 77.5 jit_solution(12884974456608171141)
XLA Ops:
  1.3 1.6 %shard_map.93 = (f32[512,128]{1,0:T(8,128)S(1)}, f32[512,128]{1,0:T(8,128)S(1)}, f32[2,2,128]{2,1,0:T(2,128)S(1)}) custom-call(s32[1]{0:T(128)S(6)} %copy.10.counts, bf16[1,4,1,32,3584]{4,3,2,1,0:T(8,128)(2,1)} %grads.1, f32[1,2,56]{2,1,0:T(2,128)} %master.1, f32[1,2,56]{2,1,0:T(2,128)} %moment1.1, f32[1,2,56]{2,1,0:T(2,128)} %moment2.1), custom_call_target="tpu_custom_call" | custom-call | tf_op jit(solution)/shard_map/pallas_call | solution.py:140
  2.9 1.9 %collective-permute-start = (f32[512,128]{1,0:T(8,128)S(1)}, f32[512,128]{1,0:T(8,128)S(1)}, u32[]{:S(2)}, u32[]{:S(2)}) collective-permute-start(f32[512,128]{1,0:T(8,128)S(1)} %get-tuple-element.12), channel_id=1, source_target_pairs={{0,128},{128,0},{1,129},{129,1},{2,130},{130,2},{3,131},{131,3},{4... | collective-permute-start | bytes 786440 | tf_op jit(solution)/shard_map/ppermute | solution.py:153
  5.4 0.9 %collective-permute-done.y = f32[512,128]{1,0:T(8,128)S(1)} collective-permute-done((f32[512,128]{1,0:T(8,128)S(1)}, f32[512,128]{1,0:T(8,128)S(1)}, u32[]{:S(2)}, u32[]{:S(2)}) %collective-permute-start) | collective-permute-done | bytes 262176 | tf_op jit(solution)/shard_map/ppermute | solution.py:153
  6.3 37.4 %all_to_all.21 = f32[64,8,128]{2,1,0:T(8,128)S(1)} all-to-all(f32[64,8,128]{2,1,0:T(8,128)S(1)} %bitcast.3), channel_id=1, replica_groups=mesh['zh'=4,'core'=2,'gy'=16,'gz'=8] {'gy','zh'}, dimensions={0} | all-to-all | bytes 524288 | tf_op jit(solution)/shard_map/all_to_all | solution.py:135
  43.7 0.1 shard_map.95
  43.8 14.6 %all_to_all.22.parts = f32[96,2,128]{2,1,0:T(2,128)S(1)} all-to-all(f32[96,2,128]{2,1,0:T(2,128)S(1)} %shard_map.95), channel_id=1, replica_groups=mesh['zh'=4,'core'=2,'gy'=16,'gz'=8] {'core','gz'}, dimensions={0} | all-to-all | bytes 196608 | tf_op jit(solution)/shard_map/all_to_all | solution.py:135
  58.4 0.2 shard_map.96
  58.7 18.0 %all_to_all.23.parts = bf16[64,2,896]{2,1,0:T(2,128)(2,1)S(1)} all-to-all(bf16[64,2,896]{2,1,0:T(2,128)(2,1)S(1)} %get-tuple-element.16), channel_id=1, replica_groups=mesh['zh'=4,'core'=2,'gy'=16,'gz'=8] {'gy','zh'}, dimensions={0} | all-to-all | bytes 458752 | tf_op jit(solution)/shard_map/all_to_all | solution.py:135
  76.7 0.8 %shard_map.97 = (bf16[1,32,3584]{2,1,0:T(8,128)(2,1)}, f32[1,2,56]{2,1,0:T(2,128)}, f32[1,2,56]{2,1,0:T(2,128)}, f32[1,2,56]{2,1,0:T(2,128)}) custom-call(bf16[64,2,896]{2,1,0:T(2,128)(2,1)S(1)} %all_to_all.23.parts, f32[3,2,56]{2,1,0:T(2,128)S(1)} %get-tuple-element.17.mine), custom_call_target="tpu_custom_call" | custom-call | tf_op jit(solution)/shard_map/pallas_call | solution.py:180
  (1 shorter events, 0.0 us)
Async XLA Ops:
  2.9 3.4 %collective-permute-start = (f32[512,128]{1,0:T(8,128)S(1)}, f32[512,128]{1,0:T(8,128)S(1)}, u32[]{:S(2)}, u32[]{:S(2)}) collective-permute-start(f32[512,128]{1,0:T(8,128)S(1)} %get-tuple-element.12), channel_id=1, source_target_pairs={{0,128},{128,0},{1,129},{129,1},{2,130},{130,2},{3,131},{131,3},{4... | collective-permute-start | bytes 786440 | tf_op jit(solution)/shard_map/ppermute | solution.py:153

commit v7 on v6

--- a/solution.py
+++ b/solution.py
@@ -11,7 +11,7 @@
 SMEM = pl.BlockSpec(memory_space=pltpu.SMEM)
 HBM = pl.BlockSpec(memory_space=pltpu.HBM)
 PARAMS = pltpu.CompilerParams(vmem_limit_bytes=8 * 1024 * 1024)
-LANES, TILE, PAIRS = 128, 8, 6
+LANES, TILE, PAIRS = 128, 8, 5
 F32, BF16 = jnp.float32, jnp.bfloat16
 
 
@@ -19,43 +19,46 @@
     _, n_slots, _, rows, width = grads.shape
     spans = 2 * keep.shape[0] // (TILE * rows)
     span, lines = width // spans, width // (spans * LANES)
-    copies = [
-        pltpu.make_async_copy(grads.at[0, :, 0, :, pl.ds(z * span, span)], slots.at[:, :, pl.ds(z * span, span)], sems.at[z])
-        for z in range(spans)
+    group = min(TILE, rows // 2)
+    pieces = [(z, i) for z in range(spans) for i in range(0, rows // 2, group)]
+    copies = []
+    for n, (z, i) in enumerate(pieces):
+        at = (pl.ds(2 * i, 2 * group), pl.ds(z * span, span))
+        copies.append(pltpu.make_async_copy(grads.at[0, :, 0, *at], slots.at[:, *at], sems.at[n]))
+    later = [
+        pltpu.make_async_copy(x.at[0], small.at[i], sems.at[len(pieces) + i]) for i, x in enumerate((master, moment1, moment2))
     ]
-    later = [pltpu.make_async_copy(x.at[0], small.at[i], sems.at[spans + i]) for i, x in enumerate((master, moment1, moment2))]
     for copy in copies + later:
         copy.start()
     core = lax.axis_index("core")
     count = counts[0]
     weights = [(slot < count).astype(F32) for slot in range(n_slots)]
-    group = min(TILE, rows // 2)
-    for z in range(spans):
-        copies[z].wait()
-        at = slice(z * span, (z + 1) * span)
-        total = slots[0, :, at].astype(F32)
+    for n, (z, i) in enumerate(pieces):
+        copies[n].wait()
+        at = (slice(2 * i, 2 * (i + group)), slice(z * span, (z + 1) * span))
+        total = slots[0, *at].astype(F32)
         for slot in range(1, n_slots):
-            total = total + weights[slot] * slots[slot, :, at].astype(F32)
+            total = total + weights[slot] * slots[slot, *at].astype(F32)
         for k in range(lines):
-            acc[z * lines + k] = total[:, k * LANES : (k + 1) * LANES]
+            acc[n * lines + k] = total[:, k * LANES : (k + 1) * LANES]
         for k in range(lines):
-            for i in range(0, rows // 2, group):
-                to = pl.ds((i * spans + z) * TILE + k, group, stride=spans * TILE)
-                keep[to, :] = acc[z * lines + k, pl.ds(2 * i + core, group, stride=2), :]
-                give[to, :] = acc[z * lines + k, pl.ds(2 * i + 1 - core, group, stride=2), :]
+            to = pl.ds((i * spans + z) * TILE + k, group, stride=spans * TILE)
+            keep[to, :] = acc[n * lines + k, pl.ds(core, group, stride=2), :]
+            give[to, :] = acc[n * lines + k, pl.ds(1 - core, group, stride=2), :]
     for copy in later:
         copy.wait()
     w = small.shape[-1]
     shards[...] = jnp.zeros(shards.shape, F32)
     shards[0, :, :w] = small[0]
     shards[0, :, w : 2 * w] = small[1]
-    shards[1, :, :w] = small[2]
+    shards[1, 0:1, :w] = small[2, 0:1]
+    shards[1, 0:1, w : 2 * w] = small[2, 1:2]
 
 
 def add(tokens, x, y, shards, out, state):
     out[...] = x[...] + y[...]
     state[...] = shards[...]
-    state[1, :, LANES - 1 :] = jnp.full((2, 1), tokens[0].astype(F32))
+    state[1, 0:1, LANES - 1 :] = jnp.full((1, 1), tokens[0].astype(F32))
 
 
 def reduce_and_pack(parts, state, out):
@@ -63,10 +66,10 @@
     for j in range(TILE, parts.shape[0], TILE):
         total = total + parts[j : j + TILE, :]
     for j in range(0, out.shape[0], PAIRS):
-        for r in range(PAIRS - 2):
+        for r in range(PAIRS - 1):
             out[j + r] = total[2 * r : 2 * r + 2, :]
-        out[j + PAIRS - 2] = state[0]
-        out[j + PAIRS - 1] = state[1]
+        out[j + PAIRS - 2, 1:2, :] = state[1, 0:1, :]
+        out[j + PAIRS - 1] = state[0]
 
 
 def adam(parts, send, mine, summed, state, result):
@@ -84,11 +87,13 @@
     total = summed[...]
     for j in range(peers):
         at = slice(j * w, (j + 1) * w)
-        state[0, :, at] = parts[j * PAIRS + PAIRS - 2, :, :w]
-        state[1, :, at] = parts[j * PAIRS + PAIRS - 2, :, w : 2 * w]
-        state[2, :, at] = parts[j * PAIRS + PAIRS - 1, :, :w]
+        pair = (j + 1) * PAIRS - 1
+        state[0, :, at] = parts[pair, :, :w]
+        state[1, :, at] = parts[pair, :, w : 2 * w]
+        state[2, 0:1, at] = parts[pair - 1, 1:2, :w]
+        state[2, 1:2, at] = parts[pair - 1, 1:2, w : 2 * w]
     master, moment1, moment2 = state[0], state[1], state[2]
-    tokens = parts[PAIRS - 1, 0:1, LANES - 1 :]
+    tokens = parts[PAIRS - 2, 1:2, LANES - 1 :]
     gradient = total / tokens
     first = 0.9 * moment1 + 0.1 * gradient
     second = 0.95 * moment2 + 0.05 * gradient * gradient
@@ -144,9 +149,9 @@
         out_specs=(VMEM,) * 3,
         scratch_shapes=[
             pltpu.VMEM((n_slots, rows, width), BF16),
-            pltpu.VMEM((width // LANES, rows, LANES), F32),
+            pltpu.VMEM((width // LANES * rows // 16, 16, LANES), F32),
             pltpu.VMEM((3, 2, w), F32),
-            pltpu.SemaphoreType.DMA((width // block + 3,)),
+            pltpu.SemaphoreType.DMA((width // block * rows // 16 + 3,)),
         ],
         compiler_params=PARAMS,
     )(counts, *pinned)

time: 77.8 us -> 77.6 us (level)
  no operation moved by 1% of the time
where the time goes in v7:
time: 77.6 us; the launch traced here: 77.3 us
  blocking collectives  69.8 us (90%)
  Pallas kernels  2.77 us (4%)
  between operations  1.96 us (3%)
  starting transfers between devices  1.92 us (2%)
  waiting for transfers between devices  0.85 us (1%)
    all_to_all x3, blocking collectives, body(): exchange = lambda x, axes: lax.all_to_all(x, axes, 0, 0, tiled=True)  69.8 us
    ppermute x1, starting transfers between devices, body(): given = lax.ppermute(give, 'core', [(0, 1), (1, 0)])  1.92 us
    pallas_call x1, Pallas kernels, body(): pl.pallas_call(accumulate, out_shape=(tiles, tiles, pairs), in_specs=[SME...  1.58 us
  transfers between devices with their start and end apart: 1, of which 1 were waited for; matrix products, arithmetic and copies ran while one was open for 0% of the time, Pallas kernels for 0%

profile of v7, /device:TPU:2, one launch (start us, length us, event | category | flops | bytes accessed | tf_op | source)
XLA Modules:
  0.0 77.3 jit_solution(11138096140419967618)
XLA Ops:
  1.3 1.6 %shard_map.93 = (f32[512,128]{1,0:T(8,128)S(1)}, f32[512,128]{1,0:T(8,128)S(1)}, f32[2,2,128]{2,1,0:T(2,128)S(1)}) custom-call(s32[1]{0:T(128)S(6)} %copy.10.counts, bf16[1,4,1,32,3584]{4,3,2,1,0:T(8,128)(2,1)} %grads.1, f32[1,2,56]{2,1,0:T(2,128)} %master.1, f32[1,2,56]{2,1,0:T(2,128)} %moment1.1, f32[1,2,56]{2,1,0:T(2,128)} %moment2.1), custom_call_target="tpu_custom_call" | custom-call | tf_op jit(solution)/shard_map/pallas_call | solution.py:145
  2.9 1.9 %collective-permute-start = (f32[512,128]{1,0:T(8,128)S(1)}, f32[512,128]{1,0:T(8,128)S(1)}, u32[]{:S(2)}, u32[]{:S(2)}) collective-permute-start(f32[512,128]{1,0:T(8,128)S(1)} %get-tuple-element.12), channel_id=1, source_target_pairs={{0,128},{128,0},{1,129},{129,1},{2,130},{130,2},{3,131},{131,3},{4... | collective-permute-start | bytes 786440 | tf_op jit(solution)/shard_map/ppermute | solution.py:158
  5.4 0.9 %collective-permute-done.y = f32[512,128]{1,0:T(8,128)S(1)} collective-permute-done((f32[512,128]{1,0:T(8,128)S(1)}, f32[512,128]{1,0:T(8,128)S(1)}, u32[]{:S(2)}, u32[]{:S(2)}) %collective-permute-start) | collective-permute-done | bytes 262176 | tf_op jit(solution)/shard_map/ppermute | solution.py:158
  6.3 37.4 %all_to_all.21 = f32[64,8,128]{2,1,0:T(8,128)S(1)} all-to-all(f32[64,8,128]{2,1,0:T(8,128)S(1)} %bitcast.3), channel_id=1, replica_groups=mesh['zh'=4,'core'=2,'gy'=16,'gz'=8] {'gy','zh'}, dimensions={0} | all-to-all | bytes 524288 | tf_op jit(solution)/shard_map/all_to_all | solution.py:140
  43.7 0.1 shard_map.95
  43.8 14.4 %all_to_all.22.parts = f32[80,2,128]{2,1,0:T(2,128)S(1)} all-to-all(f32[80,2,128]{2,1,0:T(2,128)S(1)} %shard_map.95), channel_id=1, replica_groups=mesh['zh'=4,'core'=2,'gy'=16,'gz'=8] {'core','gz'}, dimensions={0} | all-to-all | bytes 163840 | tf_op jit(solution)/shard_map/all_to_all | solution.py:140
  58.2 0.3 shard_map.96
  58.4 18.1 %all_to_all.23.parts = bf16[64,2,896]{2,1,0:T(2,128)(2,1)S(1)} all-to-all(bf16[64,2,896]{2,1,0:T(2,128)(2,1)S(1)} %get-tuple-element.16), channel_id=1, replica_groups=mesh['zh'=4,'core'=2,'gy'=16,'gz'=8] {'gy','zh'}, dimensions={0} | all-to-all | bytes 458752 | tf_op jit(solution)/shard_map/all_to_all | solution.py:140
  76.5 0.8 %shard_map.97 = (bf16[1,32,3584]{2,1,0:T(8,128)(2,1)}, f32[1,2,56]{2,1,0:T(2,128)}, f32[1,2,56]{2,1,0:T(2,128)}, f32[1,2,56]{2,1,0:T(2,128)}) custom-call(bf16[64,2,896]{2,1,0:T(2,128)(2,1)S(1)} %all_to_all.23.parts, f32[3,2,56]{2,1,0:T(2,128)S(1)} %get-tuple-element.17.mine), custom_call_target="tpu_custom_call" | custom-call | tf_op jit(solution)/shard_map/pallas_call | solution.py:185
  (1 shorter events, 0.0 us)
Async XLA Ops:
  2.9 3.4 %collective-permute-start = (f32[512,128]{1,0:T(8,128)S(1)}, f32[512,128]{1,0:T(8,128)S(1)}, u32[]{:S(2)}, u32[]{:S(2)}) collective-permute-start(f32[512,128]{1,0:T(8,128)S(1)} %get-tuple-element.12), channel_id=1, source_target_pairs={{0,128},{128,0},{1,129},{129,1},{2,130},{130,2},{3,131},{131,3},{4... | collective-permute-start | bytes 786440 | tf_op jit(solution)/shard_map/ppermute | solution.py:158

commit v8 on v7

--- a/solution.py
+++ b/solution.py
@@ -1,3 +1,5 @@
+import functools
+
 import jax
 import jax.numpy as jnp
 from jax import lax
@@ -15,9 +17,8 @@
 F32, BF16 = jnp.float32, jnp.bfloat16
 
 
-def accumulate(counts, grads, master, moment1, moment2, keep, give, shards, slots, acc, small, sems):
+def accumulate(spans, counts, grads, master, moment1, moment2, keep, give, shards, slots, acc, small, sems):
     _, n_slots, _, rows, width = grads.shape
-    spans = 2 * keep.shape[0] // (TILE * rows)
     span, lines = width // spans, width // (spans * LANES)
     group = min(TILE, rows // 2)
     pieces = [(z, i) for z in range(spans) for i in range(0, rows // 2, group)]
@@ -42,7 +43,7 @@
         for k in range(lines):
             acc[n * lines + k] = total[:, k * LANES : (k + 1) * LANES]
         for k in range(lines):
-            to = pl.ds((i * spans + z) * TILE + k, group, stride=spans * TILE)
+            to = pl.ds((i * spans + z) * lines + k, group, stride=spans * lines)
             keep[to, :] = acc[n * lines + k, pl.ds(core, group, stride=2), :]
             give[to, :] = acc[n * lines + k, pl.ds(1 - core, group, stride=2), :]
     for copy in later:
@@ -61,10 +62,13 @@
     state[1, 0:1, LANES - 1 :] = jnp.full((1, 1), tokens[0].astype(F32))
 
 
-def reduce_and_pack(parts, state, out):
-    total = parts[0:TILE, :]
-    for j in range(TILE, parts.shape[0], TILE):
-        total = total + parts[j : j + TILE, :]
+def reduce_and_pack(lines, parts, state, out, summed):
+    for k in range(lines):
+        total = parts[pl.ds(k, TILE, stride=lines), :]
+        for j in range(TILE * lines, parts.shape[0], TILE * lines):
+            total = total + parts[pl.ds(j + k, TILE, stride=lines), :]
+        summed[k : k + 1, :] = jnp.sum(total, axis=0, keepdims=True)
+    total = summed[...]
     for j in range(0, out.shape[0], PAIRS):
         for r in range(PAIRS - 1):
             out[j + r] = total[2 * r : 2 * r + 2, :]
@@ -140,10 +144,10 @@
     exchange = lambda x, axes: lax.all_to_all(x, axes, 0, 0, tiled=True)
     pinned = [pltpu.with_memory_space_constraint(x, pltpu.HBM) for x in (grads, master, moment1, moment2)]
 
-    tiles = jax.ShapeDtypeStruct((n_plane * TILE, LANES), F32)
+    tiles = jax.ShapeDtypeStruct((n_plane * block // LANES, LANES), F32)
     pairs = jax.ShapeDtypeStruct((2, 2, LANES), F32)
     keep, give, shards = pl.pallas_call(
-        accumulate,
+        functools.partial(accumulate, width // block),
         out_shape=(tiles, tiles, pairs),
         in_specs=[SMEM] + [HBM] * 4,
         out_specs=(VMEM,) * 3,
@@ -163,12 +167,13 @@
         out_specs=(VMEM, VMEM),
         compiler_params=PARAMS,
     )(total_tokens, keep, given, shards)
-    parts = exchange(parts, PLANE)
+    parts = exchange(parts.reshape(-1, 1, LANES), PLANE).reshape(parts.shape)
     packed = pl.pallas_call(
-        reduce_and_pack,
+        functools.partial(reduce_and_pack, block // LANES),
         out_shape=jax.ShapeDtypeStruct((n_line * PAIRS, 2, LANES), F32),
         in_specs=[VMEM, VMEM],
         out_specs=VMEM,
+        scratch_shapes=[pltpu.VMEM((TILE, LANES), F32)],
         compiler_params=PARAMS,
     )(parts, state)
     packed = exchange(packed, LINE)

time: 77.6 us -> 76.7 us (0.988)
  no operation moved by 1% of the time
where the time goes in v8:
time: 76.7 us; the launch traced here: 76.4 us
  blocking collectives  69.1 us (90%)
  Pallas kernels  2.62 us (3%)
  between operations  1.96 us (3%)
  starting transfers between devices  1.92 us (3%)
  waiting for transfers between devices  0.81 us (1%)
    all_to_all x3, blocking collectives, body(): exchange = lambda x, axes: lax.all_to_all(x, axes, 0, 0, tiled=True)  69.1 us
    ppermute x1, starting transfers between devices, body(): given = lax.ppermute(give, 'core', [(0, 1), (1, 0)])  1.92 us
  transfers between devices with their start and end apart: 1, of which 1 were waited for; matrix products, arithmetic and copies ran while one was open for 0% of the time, Pallas kernels for 0%

profile of v8, /device:TPU:2, one launch (start us, length us, event | category | flops | bytes accessed | tf_op | source)
XLA Modules:
  0.0 76.4 jit_solution(812044475194063426)
XLA Ops:
  1.3 1.5 %shard_map.93 = (f32[448,128]{1,0:T(8,128)S(1)}, f32[448,128]{1,0:T(8,128)S(1)}, f32[2,2,128]{2,1,0:T(2,128)S(1)}) custom-call(s32[1]{0:T(128)S(6)} %copy.11.counts, bf16[1,4,1,32,3584]{4,3,2,1,0:T(8,128)(2,1)} %grads.1, f32[1,2,56]{2,1,0:T(2,128)} %master.1, f32[1,2,56]{2,1,0:T(2,128)} %moment1.1, f32[1,2,56]{2,1,0:T(2,128)} %moment2.1), custom_call_target="tpu_custom_call" | custom-call | tf_op jit(solution)/shard_map/pallas_call | solution.py:149
  2.8 1.9 %collective-permute-start = (f32[448,128]{1,0:T(8,128)S(1)}, f32[448,128]{1,0:T(8,128)S(1)}, u32[]{:S(2)}, u32[]{:S(2)}) collective-permute-start(f32[448,128]{1,0:T(8,128)S(1)} %get-tuple-element.12), channel_id=1, source_target_pairs={{0,128},{128,0},{1,129},{129,1},{2,130},{130,2},{3,131},{131,3},{4... | collective-permute-start | bytes 688136 | tf_op jit(solution)/shard_map/ppermute | solution.py:162
  5.3 0.8 %collective-permute-done.y = f32[448,128]{1,0:T(8,128)S(1)} collective-permute-done((f32[448,128]{1,0:T(8,128)S(1)}, f32[448,128]{1,0:T(8,128)S(1)}, u32[]{:S(2)}, u32[]{:S(2)}) %collective-permute-start) | collective-permute-done | bytes 229408 | tf_op jit(solution)/shard_map/ppermute | solution.py:162
  6.2 36.8 %all_to_all.15 = f32[448,1,128]{2,1,0:T(1,128)S(1)} all-to-all(f32[448,1,128]{2,1,0:T(1,128)S(1)} %bitcast.5), channel_id=1, replica_groups=mesh['zh'=4,'core'=2,'gy'=16,'gz'=8] {'gy','zh'}, dimensions={0} | all-to-all | bytes 458752 | tf_op jit(solution)/shard_map/all_to_all | solution.py:144
  43.0 14.4 %all_to_all.16.parts = f32[80,2,128]{2,1,0:T(2,128)S(1)} all-to-all(f32[80,2,128]{2,1,0:T(2,128)S(1)} %shard_map.95), channel_id=1, replica_groups=mesh['zh'=4,'core'=2,'gy'=16,'gz'=8] {'core','gz'}, dimensions={0} | all-to-all | bytes 163840 | tf_op jit(solution)/shard_map/all_to_all | solution.py:144
  57.4 0.3 shard_map.96
  57.7 18.0 %all_to_all.17.parts = bf16[64,2,896]{2,1,0:T(2,128)(2,1)S(1)} all-to-all(bf16[64,2,896]{2,1,0:T(2,128)(2,1)S(1)} %get-tuple-element.16), channel_id=1, replica_groups=mesh['zh'=4,'core'=2,'gy'=16,'gz'=8] {'gy','zh'}, dimensions={0} | all-to-all | bytes 458752 | tf_op jit(solution)/shard_map/all_to_all | solution.py:144
  75.6 0.8 %shard_map.97 = (bf16[1,32,3584]{2,1,0:T(8,128)(2,1)}, f32[1,2,56]{2,1,0:T(2,128)}, f32[1,2,56]{2,1,0:T(2,128)}, f32[1,2,56]{2,1,0:T(2,128)}) custom-call(bf16[64,2,896]{2,1,0:T(2,128)(2,1)S(1)} %all_to_all.17.parts, f32[3,2,56]{2,1,0:T(2,128)S(1)} %get-tuple-element.17.mine), custom_call_target="tpu_custom_call" | custom-call | tf_op jit(solution)/shard_map/pallas_call | solution.py:190
  (2 shorter events, 0.1 us)
Async XLA Ops:
  2.8 3.4 %collective-permute-start = (f32[448,128]{1,0:T(8,128)S(1)}, f32[448,128]{1,0:T(8,128)S(1)}, u32[]{:S(2)}, u32[]{:S(2)}) collective-permute-start(f32[448,128]{1,0:T(8,128)S(1)} %get-tuple-element.12), channel_id=1, source_target_pairs={{0,128},{128,0},{1,129},{129,1},{2,130},{130,2},{3,131},{131,3},{4... | collective-permute-start | bytes 688136 | tf_op jit(solution)/shard_map/ppermute | solution.py:162

commit v9 on v8

--- a/solution.py
+++ b/solution.py
@@ -24,10 +24,11 @@
     pieces = [(z, i) for z in range(spans) for i in range(0, rows // 2, group)]
     copies = []
     for n, (z, i) in enumerate(pieces):
-        at = (pl.ds(2 * i, 2 * group), pl.ds(z * span, span))
-        copies.append(pltpu.make_async_copy(grads.at[0, :, 0, *at], slots.at[:, *at], sems.at[n]))
+        for h in range(2):
+            at = (pl.ds(h * n_slots // 2, n_slots // 2), pl.ds(2 * i, 2 * group), pl.ds(z * span, span))
+            copies.append(pltpu.make_async_copy(grads.at[0, at[0], 0, *at[1:]], slots.at[at], sems.at[2 * n + h]))
     later = [
-        pltpu.make_async_copy(x.at[0], small.at[i], sems.at[len(pieces) + i]) for i, x in enumerate((master, moment1, moment2))
+        pltpu.make_async_copy(x.at[0], small.at[i], sems.at[2 * len(pieces) + i]) for i, x in enumerate((master, moment1, moment2))
     ]
     for copy in copies + later:
         copy.start()
@@ -35,7 +36,8 @@
     count = counts[0]
     weights = [(slot < count).astype(F32) for slot in range(n_slots)]
     for n, (z, i) in enumerate(pieces):
-        copies[n].wait()
+        copies[2 * n].wait()
+        copies[2 * n + 1].wait()
         at = (slice(2 * i, 2 * (i + group)), slice(z * span, (z + 1) * span))
         total = slots[0, *at].astype(F32)
         for slot in range(1, n_slots):
@@ -56,10 +58,17 @@
     shards[1, 0:1, w : 2 * w] = small[2, 1:2]
 
 
+def yield_links(nanos):
+    @pl.when(lax.axis_index("core") == 1)
+    def _():
+        pl.delay(nanos)
+
+
 def add(tokens, x, y, shards, out, state):
     out[...] = x[...] + y[...]
     state[...] = shards[...]
     state[1, 0:1, LANES - 1 :] = jnp.full((1, 1), tokens[0].astype(F32))
+    yield_links(600)
 
 
 def reduce_and_pack(lines, parts, state, out, summed):
@@ -117,6 +126,8 @@
             for i in range(3):
                 mine[i] = result[i, :, j * w : (j + 1) * w]
 
+    yield_links(900)
+
 
 def assemble(parts, mine, params, master_out, moment1_out, moment2_out, whole, sems):
     _, _, block = parts.shape
@@ -155,7 +166,7 @@
             pltpu.VMEM((n_slots, rows, width), BF16),
             pltpu.VMEM((width // LANES * rows // 16, 16, LANES), F32),
             pltpu.VMEM((3, 2, w), F32),
-            pltpu.SemaphoreType.DMA((width // block * rows // 16 + 3,)),
+            pltpu.SemaphoreType.DMA((2 * (width // block * rows // 16) + 3,)),
         ],
         compiler_params=PARAMS,
     )(counts, *pinned)

time: 76.7 us -> 78.2 us (1.020)
  the two profiles are of different devices: /device:TPU:2 before, /device:TPU:16 now
where the time goes in v9:
time: 78.2 us; the launch traced here: 77.9 us
  blocking collectives  70.6 us (90%)
  Pallas kernels  2.64 us (3%)
  between operations  1.96 us (3%)
  starting transfers between devices  1.92 us (2%)
  waiting for transfers between devices  0.81 us (1%)
    all_to_all x3, blocking collectives, body(): exchange = lambda x, axes: lax.all_to_all(x, axes, 0, 0, tiled=True)  70.6 us
    ppermute x1, starting transfers between devices, body(): given = lax.ppermute(give, 'core', [(0, 1), (1, 0)])  1.92 us
  transfers between devices with their start and end apart: 1, of which 1 were waited for; matrix products, arithmetic and copies ran while one was open for 0% of the time, Pallas kernels for 0%

profile of v9, /device:TPU:16, one launch (start us, length us, event | category | flops | bytes accessed | tf_op | source)
XLA Modules:
  0.0 77.9 jit_solution(16229872365906918073)
XLA Ops:
  1.3 1.5 %shard_map.93 = (f32[448,128]{1,0:T(8,128)S(1)}, f32[448,128]{1,0:T(8,128)S(1)}, f32[2,2,128]{2,1,0:T(2,128)S(1)}) custom-call(s32[1]{0:T(128)S(6)} %copy.11.counts, bf16[1,4,1,32,3584]{4,3,2,1,0:T(8,128)(2,1)} %grads.1, f32[1,2,56]{2,1,0:T(2,128)} %master.1, f32[1,2,56]{2,1,0:T(2,128)} %moment1.1, f32[1,2,56]{2,1,0:T(2,128)} %moment2.1), custom_call_target="tpu_custom_call" | custom-call | tf_op jit(solution)/shard_map/pallas_call | solution.py:160
  2.8 1.9 %collective-permute-start = (f32[448,128]{1,0:T(8,128)S(1)}, f32[448,128]{1,0:T(8,128)S(1)}, u32[]{:S(2)}, u32[]{:S(2)}) collective-permute-start(f32[448,128]{1,0:T(8,128)S(1)} %get-tuple-element.12), channel_id=1, source_target_pairs={{0,128},{128,0},{1,129},{129,1},{2,130},{130,2},{3,131},{131,3},{4... | collective-permute-start | bytes 688136 | tf_op jit(solution)/shard_map/ppermute | solution.py:173
  5.3 0.8 %collective-permute-done.y = f32[448,128]{1,0:T(8,128)S(1)} collective-permute-done((f32[448,128]{1,0:T(8,128)S(1)}, f32[448,128]{1,0:T(8,128)S(1)}, u32[]{:S(2)}, u32[]{:S(2)}) %collective-permute-start) | collective-permute-done | bytes 229408 | tf_op jit(solution)/shard_map/ppermute | solution.py:173
  6.2 37.0 %all_to_all.15 = f32[448,1,128]{2,1,0:T(1,128)S(1)} all-to-all(f32[448,1,128]{2,1,0:T(1,128)S(1)} %bitcast.5), channel_id=1, replica_groups=mesh['zh'=4,'core'=2,'gy'=16,'gz'=8] {'gy','zh'}, dimensions={0} | all-to-all | bytes 458752 | tf_op jit(solution)/shard_map/all_to_all | solution.py:155
  43.3 14.8 %all_to_all.16.parts = f32[80,2,128]{2,1,0:T(2,128)S(1)} all-to-all(f32[80,2,128]{2,1,0:T(2,128)S(1)} %shard_map.95), channel_id=1, replica_groups=mesh['zh'=4,'core'=2,'gy'=16,'gz'=8] {'core','gz'}, dimensions={0} | all-to-all | bytes 163840 | tf_op jit(solution)/shard_map/all_to_all | solution.py:155
  58.1 0.3 shard_map.96
  58.4 18.7 %all_to_all.17.parts = bf16[64,2,896]{2,1,0:T(2,128)(2,1)S(1)} all-to-all(bf16[64,2,896]{2,1,0:T(2,128)(2,1)S(1)} %get-tuple-element.16), channel_id=1, replica_groups=mesh['zh'=4,'core'=2,'gy'=16,'gz'=8] {'gy','zh'}, dimensions={0} | all-to-all | bytes 458752 | tf_op jit(solution)/shard_map/all_to_all | solution.py:155
  77.1 0.8 %shard_map.97 = (bf16[1,32,3584]{2,1,0:T(8,128)(2,1)}, f32[1,2,56]{2,1,0:T(2,128)}, f32[1,2,56]{2,1,0:T(2,128)}, f32[1,2,56]{2,1,0:T(2,128)}) custom-call(bf16[64,2,896]{2,1,0:T(2,128)(2,1)S(1)} %all_to_all.17.parts, f32[3,2,56]{2,1,0:T(2,128)S(1)} %get-tuple-element.17.mine), custom_call_target="tpu_custom_call" | custom-call | tf_op jit(solution)/shard_map/pallas_call | solution.py:201
  (2 shorter events, 0.1 us)
Async XLA Ops:
  2.8 3.4 %collective-permute-start = (f32[448,128]{1,0:T(8,128)S(1)}, f32[448,128]{1,0:T(8,128)S(1)}, u32[]{:S(2)}, u32[]{:S(2)}) collective-permute-start(f32[448,128]{1,0:T(8,128)S(1)} %get-tuple-element.12), channel_id=1, source_target_pairs={{0,128},{128,0},{1,129},{129,1},{2,130},{130,2},{3,131},{131,3},{4... | collective-permute-start | bytes 688136 | tf_op jit(solution)/shard_map/ppermute | solution.py:173

commit v10 on v8

--- a/solution.py
+++ b/solution.py
@@ -41,7 +41,7 @@
         for slot in range(1, n_slots):
             total = total + weights[slot] * slots[slot, *at].astype(F32)
         for k in range(lines):
-            acc[n * lines + k] = total[:, k * LANES : (k + 1) * LANES]
+            acc[n * lines + k, : 2 * group] = total[:, k * LANES : (k + 1) * LANES]
         for k in range(lines):
             to = pl.ds((i * spans + z) * lines + k, group, stride=spans * lines)
             keep[to, :] = acc[n * lines + k, pl.ds(core, group, stride=2), :]
@@ -153,7 +153,7 @@
         out_specs=(VMEM,) * 3,
         scratch_shapes=[
             pltpu.VMEM((n_slots, rows, width), BF16),
-            pltpu.VMEM((width // LANES * rows // 16, 16, LANES), F32),
+            pltpu.VMEM((width // LANES * rows // 16, 24, LANES), F32),
             pltpu.VMEM((3, 2, w), F32),
             pltpu.SemaphoreType.DMA((width // block * rows // 16 + 3,)),
         ],

time: 76.7 us -> 76.7 us (level)
  no operation moved by 1% of the time
where the time goes in v10:
time: 76.7 us; the launch traced here: 76.4 us
  blocking collectives  69.1 us (90%)
  Pallas kernels  2.62 us (3%)
  between operations  1.96 us (3%)
  starting transfers between devices  1.92 us (3%)
  waiting for transfers between devices  0.81 us (1%)
    all_to_all x3, blocking collectives, body(): exchange = lambda x, axes: lax.all_to_all(x, axes, 0, 0, tiled=True)  69.1 us
    ppermute x1, starting transfers between devices, body(): given = lax.ppermute(give, 'core', [(0, 1), (1, 0)])  1.92 us
  transfers between devices with their start and end apart: 1, of which 1 were waited for; matrix products, arithmetic and copies ran while one was open for 0% of the time, Pallas kernels for 0%

profile of v10, /device:TPU:2, one launch (start us, length us, event | category | flops | bytes accessed | tf_op | source)
XLA Modules:
  0.0 76.4 jit_solution(10080178607933720279)
XLA Ops:
  1.3 1.5 %shard_map.93 = (f32[448,128]{1,0:T(8,128)S(1)}, f32[448,128]{1,0:T(8,128)S(1)}, f32[2,2,128]{2,1,0:T(2,128)S(1)}) custom-call(s32[1]{0:T(128)S(6)} %copy.11.counts, bf16[1,4,1,32,3584]{4,3,2,1,0:T(8,128)(2,1)} %grads.1, f32[1,2,56]{2,1,0:T(2,128)} %master.1, f32[1,2,56]{2,1,0:T(2,128)} %moment1.1, f32[1,2,56]{2,1,0:T(2,128)} %moment2.1), custom_call_target="tpu_custom_call" | custom-call | tf_op jit(solution)/shard_map/pallas_call | solution.py:149
  2.8 1.9 %collective-permute-start = (f32[448,128]{1,0:T(8,128)S(1)}, f32[448,128]{1,0:T(8,128)S(1)}, u32[]{:S(2)}, u32[]{:S(2)}) collective-permute-start(f32[448,128]{1,0:T(8,128)S(1)} %get-tuple-element.12), channel_id=1, source_target_pairs={{0,128},{128,0},{1,129},{129,1},{2,130},{130,2},{3,131},{131,3},{4... | collective-permute-start | bytes 688136 | tf_op jit(solution)/shard_map/ppermute | solution.py:162
  5.3 0.8 %collective-permute-done.y = f32[448,128]{1,0:T(8,128)S(1)} collective-permute-done((f32[448,128]{1,0:T(8,128)S(1)}, f32[448,128]{1,0:T(8,128)S(1)}, u32[]{:S(2)}, u32[]{:S(2)}) %collective-permute-start) | collective-permute-done | bytes 229408 | tf_op jit(solution)/shard_map/ppermute | solution.py:162
  6.2 36.8 %all_to_all.15 = f32[448,1,128]{2,1,0:T(1,128)S(1)} all-to-all(f32[448,1,128]{2,1,0:T(1,128)S(1)} %bitcast.5), channel_id=1, replica_groups=mesh['zh'=4,'core'=2,'gy'=16,'gz'=8] {'gy','zh'}, dimensions={0} | all-to-all | bytes 458752 | tf_op jit(solution)/shard_map/all_to_all | solution.py:144
  43.0 14.4 %all_to_all.16.parts = f32[80,2,128]{2,1,0:T(2,128)S(1)} all-to-all(f32[80,2,128]{2,1,0:T(2,128)S(1)} %shard_map.95), channel_id=1, replica_groups=mesh['zh'=4,'core'=2,'gy'=16,'gz'=8] {'core','gz'}, dimensions={0} | all-to-all | bytes 163840 | tf_op jit(solution)/shard_map/all_to_all | solution.py:144
  57.4 0.3 shard_map.96
  57.7 18.0 %all_to_all.17.parts = bf16[64,2,896]{2,1,0:T(2,128)(2,1)S(1)} all-to-all(bf16[64,2,896]{2,1,0:T(2,128)(2,1)S(1)} %get-tuple-element.16), channel_id=1, replica_groups=mesh['zh'=4,'core'=2,'gy'=16,'gz'=8] {'gy','zh'}, dimensions={0} | all-to-all | bytes 458752 | tf_op jit(solution)/shard_map/all_to_all | solution.py:144
  75.6 0.8 %shard_map.97 = (bf16[1,32,3584]{2,1,0:T(8,128)(2,1)}, f32[1,2,56]{2,1,0:T(2,128)}, f32[1,2,56]{2,1,0:T(2,128)}, f32[1,2,56]{2,1,0:T(2,128)}) custom-call(bf16[64,2,896]{2,1,0:T(2,128)(2,1)S(1)} %all_to_all.17.parts, f32[3,2,56]{2,1,0:T(2,128)S(1)} %get-tuple-element.17.mine), custom_call_target="tpu_custom_call" | custom-call | tf_op jit(solution)/shard_map/pallas_call | solution.py:190
  (2 shorter events, 0.1 us)
Async XLA Ops:
  2.8 3.4 %collective-permute-start = (f32[448,128]{1,0:T(8,128)S(1)}, f32[448,128]{1,0:T(8,128)S(1)}, u32[]{:S(2)}, u32[]{:S(2)}) collective-permute-start(f32[448,128]{1,0:T(8,128)S(1)} %get-tuple-element.12), channel_id=1, source_target_pairs={{0,128},{128,0},{1,129},{129,1},{2,130},{130,2},{3,131},{131,3},{4... | collective-permute-start | bytes 688136 | tf_op jit(solution)/shard_map/ppermute | solution.py:162

commit v11 on v10

--- a/solution.py
+++ b/solution.py
@@ -118,21 +118,19 @@
                 mine[i] = result[i, :, j * w : (j + 1) * w]
 
 
-def assemble(parts, mine, params, master_out, moment1_out, moment2_out, whole, sems):
+def assemble(parts, mine, params, master_out, moment1_out, moment2_out, sems):
     _, _, block = parts.shape
-    rows, width = whole.shape
+    rows, width = params.shape[1:]
     spans = width // block
     outs = [pltpu.make_async_copy(mine.at[i], x.at[0], sems.at[i]) for i, x in enumerate((master_out, moment1_out, moment2_out))]
     for copy in outs:
         copy.start()
-    for t in range(rows // 8):
-        for i in range(4 * t, 4 * t + 4):
-            for z in range(spans):
-                whole[2 * i : 2 * i + 2, z * block : (z + 1) * block] = parts[i * spans + z]
-        at = pl.ds(8 * t, 8)
-        copy = pltpu.make_async_copy(whole.at[at], params.at[0, at], sems.at[3 + t])
-        copy.start()
-        outs.append(copy)
+    for i in range(rows // 2):
+        for z in range(spans):
+            at = (pl.ds(2 * i, 2), pl.ds(z * block, block))
+            copy = pltpu.make_async_copy(parts.at[i * spans + z], params.at[0, *at], sems.at[3 + i * spans + z])
+            copy.start()
+            outs.append(copy)
     for copy in outs:
         copy.wait()
 
@@ -192,7 +190,7 @@
         out_shape=(jax.ShapeDtypeStruct((1, rows, width), BF16), shard, shard, shard),
         in_specs=[VMEM, VMEM],
         out_specs=(HBM,) * 4,
-        scratch_shapes=[pltpu.VMEM((rows, width), BF16), pltpu.SemaphoreType.DMA((3 + rows // 8,))],
+        scratch_shapes=[pltpu.SemaphoreType.DMA((3 + n_plane,))],
         compiler_params=PARAMS,
     )(gathered, mine)
 

time: 76.7 us -> 77.3 us (level)
  no operation moved by 1% of the time
where the time goes in v11:
time: 77.3 us; the launch traced here: 77 us
  blocking collectives  69.1 us (89%)
  Pallas kernels  3.22 us (4%)
  between operations  1.96 us (3%)
  starting transfers between devices  1.92 us (2%)
  waiting for transfers between devices  0.81 us (1%)
    all_to_all x3, blocking collectives, body(): exchange = lambda x, axes: lax.all_to_all(x, axes, 0, 0, tiled=True)  69.1 us
    ppermute x1, starting transfers between devices, body(): given = lax.ppermute(give, 'core', [(0, 1), (1, 0)])  1.92 us
  transfers between devices with their start and end apart: 1, of which 1 were waited for; matrix products, arithmetic and copies ran while one was open for 0% of the time, Pallas kernels for 0%

profile of v11, /device:TPU:2, one launch (start us, length us, event | category | flops | bytes accessed | tf_op | source)
XLA Modules:
  0.0 77.0 jit_solution(9955382379964186507)
XLA Ops:
  1.3 1.5 %shard_map.93 = (f32[448,128]{1,0:T(8,128)S(1)}, f32[448,128]{1,0:T(8,128)S(1)}, f32[2,2,128]{2,1,0:T(2,128)S(1)}) custom-call(s32[1]{0:T(128)S(6)} %copy.11.counts, bf16[1,4,1,32,3584]{4,3,2,1,0:T(8,128)(2,1)} %grads.1, f32[1,2,56]{2,1,0:T(2,128)} %master.1, f32[1,2,56]{2,1,0:T(2,128)} %moment1.1, f32[1,2,56]{2,1,0:T(2,128)} %moment2.1), custom_call_target="tpu_custom_call" | custom-call | tf_op jit(solution)/shard_map/pallas_call | solution.py:147
  2.8 1.9 %collective-permute-start = (f32[448,128]{1,0:T(8,128)S(1)}, f32[448,128]{1,0:T(8,128)S(1)}, u32[]{:S(2)}, u32[]{:S(2)}) collective-permute-start(f32[448,128]{1,0:T(8,128)S(1)} %get-tuple-element.12), channel_id=1, source_target_pairs={{0,128},{128,0},{1,129},{129,1},{2,130},{130,2},{3,131},{131,3},{4... | collective-permute-start | bytes 688136 | tf_op jit(solution)/shard_map/ppermute | solution.py:160
  5.3 0.8 %collective-permute-done.y = f32[448,128]{1,0:T(8,128)S(1)} collective-permute-done((f32[448,128]{1,0:T(8,128)S(1)}, f32[448,128]{1,0:T(8,128)S(1)}, u32[]{:S(2)}, u32[]{:S(2)}) %collective-permute-start) | collective-permute-done | bytes 229408 | tf_op jit(solution)/shard_map/ppermute | solution.py:160
  6.2 36.8 %all_to_all.15 = f32[448,1,128]{2,1,0:T(1,128)S(1)} all-to-all(f32[448,1,128]{2,1,0:T(1,128)S(1)} %bitcast.5), channel_id=1, replica_groups=mesh['zh'=4,'core'=2,'gy'=16,'gz'=8] {'gy','zh'}, dimensions={0} | all-to-all | bytes 458752 | tf_op jit(solution)/shard_map/all_to_all | solution.py:142
  43.0 14.4 %all_to_all.16.parts = f32[80,2,128]{2,1,0:T(2,128)S(1)} all-to-all(f32[80,2,128]{2,1,0:T(2,128)S(1)} %shard_map.95), channel_id=1, replica_groups=mesh['zh'=4,'core'=2,'gy'=16,'gz'=8] {'core','gz'}, dimensions={0} | all-to-all | bytes 163840 | tf_op jit(solution)/shard_map/all_to_all | solution.py:142
  57.4 0.3 shard_map.96
  57.7 18.0 %all_to_all.17.parts = bf16[64,2,896]{2,1,0:T(2,128)(2,1)S(1)} all-to-all(bf16[64,2,896]{2,1,0:T(2,128)(2,1)S(1)} %get-tuple-element.16), channel_id=1, replica_groups=mesh['zh'=4,'core'=2,'gy'=16,'gz'=8] {'gy','zh'}, dimensions={0} | all-to-all | bytes 458752 | tf_op jit(solution)/shard_map/all_to_all | solution.py:142
  75.6 1.4 %shard_map.97 = (bf16[1,32,3584]{2,1,0:T(8,128)(2,1)}, f32[1,2,56]{2,1,0:T(2,128)}, f32[1,2,56]{2,1,0:T(2,128)}, f32[1,2,56]{2,1,0:T(2,128)}) custom-call(bf16[64,2,896]{2,1,0:T(2,128)(2,1)S(1)} %all_to_all.17.parts, f32[3,2,56]{2,1,0:T(2,128)S(1)} %get-tuple-element.17.mine), custom_call_target="tpu_custom_call" | custom-call | tf_op jit(solution)/shard_map/pallas_call | solution.py:188
  (2 shorter events, 0.1 us)
Async XLA Ops:
  2.8 3.4 %collective-permute-start = (f32[448,128]{1,0:T(8,128)S(1)}, f32[448,128]{1,0:T(8,128)S(1)}, u32[]{:S(2)}, u32[]{:S(2)}) collective-permute-start(f32[448,128]{1,0:T(8,128)S(1)} %get-tuple-element.12), channel_id=1, source_target_pairs={{0,128},{128,0},{1,129},{129,1},{2,130},{130,2},{3,131},{131,3},{4... | collective-permute-start | bytes 688136 | tf_op jit(solution)/shard_map/ppermute | solution.py:160

commit v12 on v10

--- a/solution.py
+++ b/solution.py
@@ -29,7 +29,7 @@
     later = [
         pltpu.make_async_copy(x.at[0], small.at[i], sems.at[len(pieces) + i]) for i, x in enumerate((master, moment1, moment2))
     ]
-    for copy in copies + later:
+    for copy in later + copies:
         copy.start()
     core = lax.axis_index("core")
     count = counts[0]

time: 76.7 us -> 76.8 us (level)
  no operation moved by 1% of the time
where the time goes in v12:
time: 76.8 us; the launch traced here: 76.5 us
  blocking collectives  69.1 us (90%)
  Pallas kernels  2.66 us (3%)
  between operations  1.96 us (3%)
  starting transfers between devices  1.92 us (2%)
  waiting for transfers between devices  0.81 us (1%)
    all_to_all x3, blocking collectives, body(): exchange = lambda x, axes: lax.all_to_all(x, axes, 0, 0, tiled=True)  69.1 us
    ppermute x1, starting transfers between devices, body(): given = lax.ppermute(give, 'core', [(0, 1), (1, 0)])  1.92 us
  transfers between devices with their start and end apart: 1, of which 1 were waited for; matrix products, arithmetic and copies ran while one was open for 0% of the time, Pallas kernels for 0%

profile of v12, /device:TPU:2, one launch (start us, length us, event | category | flops | bytes accessed | tf_op | source)
XLA Modules:
  0.0 76.5 jit_solution(1331831422734170851)
XLA Ops:
  1.3 1.5 %shard_map.93 = (f32[448,128]{1,0:T(8,128)S(1)}, f32[448,128]{1,0:T(8,128)S(1)}, f32[2,2,128]{2,1,0:T(2,128)S(1)}) custom-call(s32[1]{0:T(128)S(6)} %copy.11.counts, bf16[1,4,1,32,3584]{4,3,2,1,0:T(8,128)(2,1)} %grads.1, f32[1,2,56]{2,1,0:T(2,128)} %master.1, f32[1,2,56]{2,1,0:T(2,128)} %moment1.1, f32[1,2,56]{2,1,0:T(2,128)} %moment2.1), custom_call_target="tpu_custom_call" | custom-call | tf_op jit(solution)/shard_map/pallas_call | solution.py:149
  2.8 1.9 %collective-permute-start = (f32[448,128]{1,0:T(8,128)S(1)}, f32[448,128]{1,0:T(8,128)S(1)}, u32[]{:S(2)}, u32[]{:S(2)}) collective-permute-start(f32[448,128]{1,0:T(8,128)S(1)} %get-tuple-element.12), channel_id=1, source_target_pairs={{0,128},{128,0},{1,129},{129,1},{2,130},{130,2},{3,131},{131,3},{4... | collective-permute-start | bytes 688136 | tf_op jit(solution)/shard_map/ppermute | solution.py:162
  5.4 0.8 %collective-permute-done.y = f32[448,128]{1,0:T(8,128)S(1)} collective-permute-done((f32[448,128]{1,0:T(8,128)S(1)}, f32[448,128]{1,0:T(8,128)S(1)}, u32[]{:S(2)}, u32[]{:S(2)}) %collective-permute-start) | collective-permute-done | bytes 229408 | tf_op jit(solution)/shard_map/ppermute | solution.py:162
  6.2 36.8 %all_to_all.15 = f32[448,1,128]{2,1,0:T(1,128)S(1)} all-to-all(f32[448,1,128]{2,1,0:T(1,128)S(1)} %bitcast.5), channel_id=1, replica_groups=mesh['zh'=4,'core'=2,'gy'=16,'gz'=8] {'gy','zh'}, dimensions={0} | all-to-all | bytes 458752 | tf_op jit(solution)/shard_map/all_to_all | solution.py:144
  43.0 14.4 %all_to_all.16.parts = f32[80,2,128]{2,1,0:T(2,128)S(1)} all-to-all(f32[80,2,128]{2,1,0:T(2,128)S(1)} %shard_map.95), channel_id=1, replica_groups=mesh['zh'=4,'core'=2,'gy'=16,'gz'=8] {'core','gz'}, dimensions={0} | all-to-all | bytes 163840 | tf_op jit(solution)/shard_map/all_to_all | solution.py:144
  57.4 0.3 shard_map.96
  57.7 18.0 %all_to_all.17.parts = bf16[64,2,896]{2,1,0:T(2,128)(2,1)S(1)} all-to-all(bf16[64,2,896]{2,1,0:T(2,128)(2,1)S(1)} %get-tuple-element.16), channel_id=1, replica_groups=mesh['zh'=4,'core'=2,'gy'=16,'gz'=8] {'gy','zh'}, dimensions={0} | all-to-all | bytes 458752 | tf_op jit(solution)/shard_map/all_to_all | solution.py:144
  75.6 0.8 %shard_map.97 = (bf16[1,32,3584]{2,1,0:T(8,128)(2,1)}, f32[1,2,56]{2,1,0:T(2,128)}, f32[1,2,56]{2,1,0:T(2,128)}, f32[1,2,56]{2,1,0:T(2,128)}) custom-call(bf16[64,2,896]{2,1,0:T(2,128)(2,1)S(1)} %all_to_all.17.parts, f32[3,2,56]{2,1,0:T(2,128)S(1)} %get-tuple-element.17.mine), custom_call_target="tpu_custom_call" | custom-call | tf_op jit(solution)/shard_map/pallas_call | solution.py:190
  (2 shorter events, 0.1 us)
Async XLA Ops:
  2.8 3.4 %collective-permute-start = (f32[448,128]{1,0:T(8,128)S(1)}, f32[448,128]{1,0:T(8,128)S(1)}, u32[]{:S(2)}, u32[]{:S(2)}) collective-permute-start(f32[448,128]{1,0:T(8,128)S(1)} %get-tuple-element.12), channel_id=1, source_target_pairs={{0,128},{128,0},{1,129},{129,1},{2,130},{130,2},{3,131},{131,3},{4... | collective-permute-start | bytes 688136 | tf_op jit(solution)/shard_map/ppermute | solution.py:162
